TPU v7x, 512 devices: a whole 4x4x16 slice. The times are simulated.
512 devices in a mesh: dp: 4 (over y_lo, core), lat: 16 (over z), chan: 8 (over y_hi, x).
Axes of the slice: x: 4, y: 4 (y_hi: 2, y_lo: 2; y = y_hi * 2 + y_lo), z: 16, core: 2. Of those that a mesh axis runs over, the one named last changes fastest.
Arguments:
- saved_input: bfloat16 [4, 64, 720, 1024], P('dp', None, 'lat', 'chan'), may hold values from -6 to 6
- grad_output: bfloat16 [4, 64, 720, 1024], P('dp', None, 'lat', 'chan'), may hold values from -6 to 6
- legendre: bfloat16 [64, 192, 720], P('lat'), may hold values from -0.21875 to 0.21875
- quad_weight: float32 [720], replicated, may hold values from 0.3 to 3
- mixing_weight: bfloat16 [192, 512, 1024], P('lat', None, 'chan'), may hold values from -0.375 to 0.375
Outputs:
- grad_weight: bfloat16 [192, 512, 1024], P('lat', 'dp', 'chan')
- grad_input: bfloat16 [4, 64, 720, 1024], P('dp', None, 'lat', 'chan')
All inputs are finite; a program needn't handle non-finite values.
Results may differ from a plain program's by a relative error of at most 0.014.
Values may be sent and summed in bfloat16 or wider, within the bound.
A program may use at most 64 MiB of HBM per device.

v0:
```python
import jax
import jax.numpy as jnp
from jax import lax
from jax.sharding import PartitionSpec as P


def side_by_side(arrays, axis, split_dim, concat_dim, along):
    ends, at = ([], 0)
    for a in arrays[:-1]:
        at += a.shape[along]
        ends.append(at)
    both = jnp.concatenate(arrays, axis=along)
    return tuple(
        jnp.split(
            lax.all_to_all(both, axis, split_axis=split_dim, concat_axis=concat_dim, tiled=True),
            ends,
            axis=along,
        )
    )


def joined_along(pieces, dim):
    lengths = list(pieces.shape[1:])
    lengths[dim] *= pieces.shape[0]
    return jnp.moveaxis(pieces, 0, dim).reshape(lengths)


def copy_for_each(value, axis):
    copies = jnp.broadcast_to(value, (lax.axis_size(axis), *value.shape))
    return lax.all_to_all(copies, axis, split_axis=0, concat_axis=0, tiled=True)


def gather_directly(value, axis, dim):
    return joined_along(copy_for_each(value, axis), dim)


def split_up(value, dim, devices):
    lengths = value.shape
    pieces = value.reshape(*lengths[:dim], devices, lengths[dim] // devices, *lengths[dim + 1 :])
    return jnp.moveaxis(pieces, dim, 0)


def summed_on_arrival(value, axis, dim):
    pieces = split_up(value, dim, lax.axis_size(axis))
    arrived = lax.all_to_all(pieces, axis, split_axis=0, concat_axis=0, tiled=True)
    return arrived.astype(jnp.float32).sum(axis=0)


def partner_of(grads):
    pairs = grads.reshape(grads.shape[:-1] + (grads.shape[-1] // 2, 2))
    swapped = jnp.stack([pairs[..., 1], -pairs[..., 0]], axis=-1)
    return swapped.reshape(grads.shape)


def weight_terms(spectra, grads):
    pairs = spectra.reshape(spectra.shape[:-1] + (spectra.shape[-1] // 2, 2))
    partner = partner_of(grads)
    first = jnp.einsum("bmli,bmlq->liq", pairs[..., 0], grads, preferred_element_type=jnp.float32)
    second = jnp.einsum(
        "bmli,bmlq->liq", pairs[..., 1], partner, preferred_element_type=jnp.float32
    )
    return first + second


def on_device(saved_input, grad_output, legendre, quad_weight, mixing_weight):
    analysis = (legendre.astype(jnp.float32) * quad_weight[None, None, :]).astype(jnp.bfloat16)
    spectra = jnp.einsum(
        "mlj,bmjq->bmlq",
        analysis,
        lax.all_to_all(saved_input, "lat", split_axis=1, concat_axis=2, tiled=True),
        preferred_element_type=jnp.float32,
    ).astype(jnp.bfloat16)
    grads = jnp.einsum(
        "mlj,bmjq->bmlq",
        legendre,
        lax.all_to_all(grad_output, "lat", split_axis=1, concat_axis=2, tiled=True),
        preferred_element_type=jnp.float32,
    ).astype(jnp.bfloat16)
    spectra, grad_spectra = (spectra, grads)
    spectra, grad_spectra = side_by_side((spectra, grad_spectra), "lat", 2, 1, 0)
    batch = saved_input.shape[0] * lax.axis_size("dp")
    complete = gather_directly(spectra, "chan", 3)
    partial_terms = weight_terms(complete, grad_spectra) / batch
    summed = summed_on_arrival(partial_terms.astype(jnp.bfloat16), "dp", 1)
    grad_weight = summed.astype(jnp.bfloat16)
    partner = partner_of(grad_spectra)
    sum_real = jnp.einsum(
        "bmlq,liq->bmli", grad_spectra, mixing_weight, preferred_element_type=jnp.float32
    )
    sum_imag = jnp.einsum(
        "bmlq,liq->bmli", partner, mixing_weight, preferred_element_type=jnp.float32
    )
    terms = jnp.stack([sum_real, sum_imag], axis=-1)
    terms = terms.reshape(terms.shape[:3] + (terms.shape[3] * 2,))
    grad_spec_in = summed_on_arrival(terms.astype(jnp.bfloat16), "chan", 3).astype(jnp.bfloat16)
    grad_local = jnp.einsum(
        "mlj,bmlq->bmjq",
        analysis,
        lax.all_to_all(grad_spec_in, "lat", split_axis=1, concat_axis=2, tiled=True),
        preferred_element_type=jnp.float32,
    ).astype(jnp.bfloat16)
    grad_input = lax.all_to_all(grad_local, "lat", split_axis=2, concat_axis=1, tiled=True)
    return (grad_weight, grad_input)


def solution(mesh):
    in_specs = (
        P("dp", None, "lat", "chan"),
        P("dp", None, "lat", "chan"),
        P("lat", None, None),
        P(),
        P("lat", None, "chan"),
    )
    out_specs = (P("lat", "dp", "chan"), P("dp", None, "lat", "chan"))
    return jax.shard_map(
        on_device, mesh=mesh, in_specs=in_specs, out_specs=out_specs, check_vma=False
    )
```

profile of v0, /device:TPU:1, one launch (start us, length us, event | category | flops | bytes accessed | tf_op | source)
XLA Modules:
  0.0 320.7 jit_solution(14644961490172514969)
XLA Ops:
  0.7 2.7 copy.77
  3.3 15.7 %all-to-all-start = ((bf16[1,64,45,128]{3,2,0,1:T(8,128)(2,1)}), bf16[1,64,45,128]{3,2,0,1:T(8,128)(2,1)S(1)}, u32[]{:S(2)}, u32[]{:S(2)}) async-start(bf16[1,64,45,128]{3,2,0,1:T(8,128)(2,1)} %copy.77), calls=%async_computation | async-start | bytes 1572864 | tf_op jit(solution)/shard_map/all_to_all | solution.py:70
  19.1 1.4 copy.80
  20.5 33.2 %all-to-all-done = bf16[1,64,45,128]{3,2,0,1:T(8,128)(2,1)S(1)} async-done(((bf16[1,64,45,128]{3,2,0,1:T(8,128)(2,1)}), bf16[1,64,45,128]{3,2,0,1:T(8,128)(2,1)S(1)}, u32[]{:S(2)}, u32[]{:S(2)}) %all-to-all-start) | async-done | bytes 737312 | tf_op jit(solution)/shard_map/all_to_all | solution.py:70
  53.7 12.1 %all-to-all-start.1 = ((bf16[1,64,45,128]{3,2,0,1:T(8,128)(2,1)}), bf16[1,64,45,128]{3,2,0,1:T(8,128)(2,1)S(1)}, u32[]{:S(2)}, u32[]{:S(2)}) async-start(bf16[1,64,45,128]{3,2,0,1:T(8,128)(2,1)} %copy.80), calls=%async_computation.1 | async-start | bytes 1572864 | tf_op jit(solution)/shard_map/all_to_all | solution.py:76
  65.8 1.1 copy.78
  67.0 33.4 %all-to-all-done.1 = bf16[1,64,45,128]{3,2,0,1:T(8,128)(2,1)S(1)} async-done(((bf16[1,64,45,128]{3,2,0,1:T(8,128)(2,1)}), bf16[1,64,45,128]{3,2,0,1:T(8,128)(2,1)S(1)}, u32[]{:S(2)}, u32[]{:S(2)}) %all-to-all-start.1) | async-done | bytes 737312 | tf_op jit(solution)/shard_map/all_to_all | solution.py:76
  100.4 0.3 copy.81
  100.7 1.8 fusion.4
  102.5 0.5 fusion.3
  103.0 0.3 copy.83
  103.4 29.7 %all_to_all.93 = bf16[2,4,192,128]{3,1,0,2:T(4,128)(2,1)S(1)} all-to-all(bf16[2,4,192,128]{3,1,0,2:T(4,128)(2,1)S(1)} %copy.83), channel_id=1, replica_groups=mesh['dp'=4,'lat'=16,'chan'=8] {'lat'}, dimensions={2} | all-to-all | bytes 786432 | tf_op jit(solution)/shard_map/all_to_all | solution.py:15
  133.2 0.1 fusion.13
  133.3 1.9 copy.90
  135.3 1.5 broadcast_in_dim.4
  136.8 6.7 %all-to-all-start.3 = ((bf16[8,1,64,12,128]{4,2,3,1,0:T(8,128)(2,1)}), bf16[8,1,64,12,128]{4,2,3,1,0:T(8,128)(2,1)S(1)}, u32[]{:S(2)}, u32[]{:S(2)}) async-start(bf16[8,1,64,12,128]{4,2,3,1,0:T(8,128)(2,1)} %broadcast_in_dim.4), calls=%async_computation.3 | async-start | bytes 3145728 | tf_op jit(solution)/shard_map/all_to_all | solution.py:30
  143.5 5.8 %fusion.12 = (bf16[1,64,12,64,1]{2,4,3,1,0:T(2,128)(2,1)S(1)}, bf16[1,64,12,64,1]{2,4,3,1,0:T(2,128)(2,1)S(1)}) fusion(bf16[1,64,12,64,2]{2,4,3,1,0:T(2,128)(2,1)} %bitcast.77), kind=kLoop, calls=%fused_computation.24 | loop fusion | flops 49152 | bytes 393216 | tf_op jit(solution)/shard_map/slice | solution.py:51
  149.3 0.8 copy.88
  150.1 6.4 %pad_maximum_fusion = bf16[1,64,12,64,2]{2,4,3,1,0:T(2,128)(2,1)} fusion(bf16[1,64,12,64,1]{2,4,3,1,0:T(2,128)(2,1)S(1)} %get-tuple-element.5, bf16[1,64,12,64,1]{2,4,3,1,0:T(2,128)(2,1)S(1)} %get-tuple-element.4), kind=kLoop, calls=%fused_computation.3 | loop fusion | flops 393216 | bytes 393216 | tf_op jit(solution)/shard_map/stack | solution.py:51
  156.5 5.1 %copy.91 = bf16[1,64,12,64,2]{1,4,3,2,0:T(2,128)(2,1)S(1)} copy(bf16[1,64,12,64,2]{2,4,3,1,0:T(2,128)(2,1)} %pad_maximum_fusion) | data formatting | bytes 393216 | tf_op jit(solution)/shard_map/stack | solution.py:51
  161.6 1.6 fusion
  163.2 0.7 fusion.1
  163.9 1.3 pad_maximum_fusion.1
  165.2 8.3 %copy.95 = bf16[1,64,12,512,2]{1,4,3,2,0:T(2,128)(2,1)} copy(bf16[1,64,12,512,2]{3,1,2,4,0:T(8,128)(2,1)} %pad_maximum_fusion.1) | data formatting | bytes 3145728 | tf_op jit(solution)/shard_map/stack | solution.py:93
  173.6 4.3 %copy.96 = bf16[8,1,64,12,128]{4,2,3,1,0:T(8,128)(2,1)} copy(bf16[8,1,64,12,128]{2,4,0,3,1:T(8,128)(2,1)} %bitcast.78) | data formatting | bytes 3145728 | tf_op jit(solution)/shard_map/transpose | solution.py:40
  177.9 1.2 copy-done.1
  179.1 6.6 %all-to-all-start.5 = ((bf16[8,1,64,12,128]{4,2,3,1,0:T(8,128)(2,1)}), bf16[8,1,64,12,128]{4,2,3,1,0:T(8,128)(2,1)S(1)}, u32[]{:S(2)}, u32[]{:S(2)}) async-start(bf16[8,1,64,12,128]{4,2,3,1,0:T(8,128)(2,1)} %copy.96), calls=%async_computation.5 | async-start | bytes 3145728 | tf_op jit(solution)/shard_map/all_to_all | solution.py:45
  185.7 4.1 %copy.86 = bf16[1,64,12,8,128]{1,4,3,2,0:T(8,128)(2,1)} copy(bf16[1,64,12,8,128]{4,1,2,0,3:T(8,128)(2,1)} %bitcast.80) | data formatting | bytes 3145728 | tf_op jit(solution)/shard_map/transpose | solution.py:25
  189.8 10.6 %all-to-all-done.5 = bf16[8,1,64,12,128]{4,2,3,1,0:T(8,128)(2,1)S(1)} async-done(((bf16[8,1,64,12,128]{4,2,3,1,0:T(8,128)(2,1)}), bf16[8,1,64,12,128]{4,2,3,1,0:T(8,128)(2,1)S(1)}, u32[]{:S(2)}, u32[]{:S(2)}) %all-to-all-start.5) | async-done | bytes 1572896 | tf_op jit(solution)/shard_map/all_to_all | solution.py:45
  200.5 1.0 reduce_sum.27
  201.4 1.1 copy.106
  202.6 1.0 copy.98
  203.6 20.5 %all-to-all-start.6 = ((bf16[1,64,12,128]{3,2,0,1:T(8,128)(2,1)}), bf16[1,64,12,128]{3,2,0,1:T(8,128)(2,1)}, u32[]{:S(2)}, u32[]{:S(2)}) async-start(bf16[1,64,12,128]{3,2,0,1:T(8,128)(2,1)} %copy.98), calls=%async_computation.6 | async-start | bytes 524288 | tf_op jit(solution)/shard_map/all_to_all | solution.py:99
  224.1 9.5 %fusion.11 = (bf16[1,64,12,512,1]{1,4,3,2,0:T(2,128)(2,1)}, bf16[1,64,12,512,1]{1,4,3,2,0:T(2,128)(2,1)}) fusion(bf16[1,64,12,512,2]{1,4,3,2,0:T(2,128)(2,1)} %bitcast.76), kind=kLoop, calls=%fused_computation.23 | loop fusion | bytes 3145728 | tf_op jit(solution)/shard_map/slice | solution.py:60
  233.6 6.6 %copy.107 = bf16[1,64,12,512,1]{3,1,2,4,0:T(8,128)(2,1)S(1)} copy(bf16[1,64,12,512,1]{1,4,3,2,0:T(2,128)(2,1)} %get-tuple-element.3) | data formatting | bytes 1572864
  240.3 6.6 %copy.108 = bf16[1,64,12,512,1]{3,1,2,4,0:T(8,128)(2,1)S(1)} copy(bf16[1,64,12,512,1]{1,4,3,2,0:T(2,128)(2,1)} %get-tuple-element.2) | data formatting | bytes 1572864
  246.9 1.6 fusion.6
  248.5 0.7 multiply_convert_fusion
  249.2 1.3 copy.116
  250.5 4.6 %all-to-all-start.4 = ((bf16[4,12,128,128]{3,2,1,0:T(8,128)(2,1)}), bf16[4,12,128,128]{3,2,1,0:T(8,128)(2,1)S(1)}, u32[]{:S(2)}, u32[]{:S(2)}) async-start(bf16[4,12,128,128]{3,2,1,0:T(8,128)(2,1)} %bitcast.79), calls=%async_computation.4 | async-start | bytes 3145728 | tf_op jit(solution)/shard_map/all_to_all | solution.py:45
  255.1 1.0 copy.99
  256.2 2.0 fusion.2
  258.1 1.1 copy.102
  259.3 14.9 %all-to-all-done.4 = bf16[4,12,128,128]{3,2,1,0:T(8,128)(2,1)S(1)} async-done(((bf16[4,12,128,128]{3,2,1,0:T(8,128)(2,1)}), bf16[4,12,128,128]{3,2,1,0:T(8,128)(2,1)S(1)}, u32[]{:S(2)}, u32[]{:S(2)}) %all-to-all-start.4) | async-done | bytes 1572896 | tf_op jit(solution)/shard_map/all_to_all | solution.py:45
  274.2 11.7 %all-to-all-start.7 = ((bf16[1,4,720,128]{3,1,0,2:T(4,128)(2,1)}), bf16[1,4,720,128]{3,1,0,2:T(4,128)(2,1)}, u32[]{:S(2)}, u32[]{:S(2)}) async-start(bf16[1,4,720,128]{3,1,0,2:T(4,128)(2,1)} %copy.102), calls=%async_computation.7 | async-start | bytes 1474560 | tf_op jit(solution)/shard_map/all_to_all | solution.py:102
  285.9 1.1 reduce_sum.26
  287.0 31.3 %all-to-all-done.7 = bf16[1,4,720,128]{3,1,0,2:T(4,128)(2,1)} async-done(((bf16[1,4,720,128]{3,1,0,2:T(4,128)(2,1)}), bf16[1,4,720,128]{3,1,0,2:T(4,128)(2,1)}, u32[]{:S(2)}, u32[]{:S(2)}) %all-to-all-start.7) | async-done | bytes 737312 | tf_op jit(solution)/shard_map/all_to_all | solution.py:102
  318.3 2.4 copy.103
  (17 shorter events, 0.4 us)
Async XLA Ops:
  0.6 161.0 %copy-start = (bf16[12,512,128]{2,1,0:T(8,128)(2,1)S(1)}, bf16[12,512,128]{2,1,0:T(8,128)(2,1)}, u32[]{:S(2)}) copy-start(bf16[12,512,128]{2,1,0:T(8,128)(2,1)} %param.9) | copy-start | bytes 4718596
  0.6 18.4 %copy-start.3 = (bf16[1,64,45,128]{3,1,2,0:T(8,128)(2,1)S(1)}, bf16[1,64,45,128]{3,1,2,0:T(8,128)(2,1)}, u32[]{:S(2)}) copy-start(bf16[1,64,45,128]{3,1,2,0:T(8,128)(2,1)} %param.6) | copy-start | bytes 2211844
  3.3 50.4 %all-to-all-start = ((bf16[1,64,45,128]{3,2,0,1:T(8,128)(2,1)}), bf16[1,64,45,128]{3,2,0,1:T(8,128)(2,1)S(1)}, u32[]{:S(2)}, u32[]{:S(2)}) async-start(bf16[1,64,45,128]{3,2,0,1:T(8,128)(2,1)} %copy.77), calls=%async_computation | async-start | bytes 1572864 | tf_op jit(solution)/shard_map/all_to_all | solution.py:70
  53.7 46.7 %all-to-all-start.1 = ((bf16[1,64,45,128]{3,2,0,1:T(8,128)(2,1)}), bf16[1,64,45,128]{3,2,0,1:T(8,128)(2,1)S(1)}, u32[]{:S(2)}, u32[]{:S(2)}) async-start(bf16[1,64,45,128]{3,2,0,1:T(8,128)(2,1)} %copy.80), calls=%async_computation.1 | async-start | bytes 1572864 | tf_op jit(solution)/shard_map/all_to_all | solution.py:76
  67.0 35.5 %copy-start.4 = (bf16[1,16,4,45,128]{4,2,3,1,0:T(4,128)(2,1)S(1)}, bf16[1,16,4,45,128]{4,2,3,1,0:T(4,128)(2,1)}, u32[]{:S(2)}) copy-start(bf16[1,16,4,45,128]{4,2,3,1,0:T(4,128)(2,1)} %copy.78) | copy-start | bytes 2211844
  67.0 35.5 %copy-start.5 = (f32[720]{0:T(1024)S(1)}, f32[720]{0:T(1024)}, u32[]{:S(2)}) copy-start(f32[720]{0:T(1024)} %param.8) | copy-start | bytes 8644
  100.4 2.1 copy-start.2
  136.8 41.1 %all-to-all-start.3 = ((bf16[8,1,64,12,128]{4,2,3,1,0:T(8,128)(2,1)}), bf16[8,1,64,12,128]{4,2,3,1,0:T(8,128)(2,1)S(1)}, u32[]{:S(2)}, u32[]{:S(2)}) async-start(bf16[8,1,64,12,128]{4,2,3,1,0:T(8,128)(2,1)} %broadcast_in_dim.4), calls=%async_computation.3 | async-start | bytes 3145728 | tf_op jit(solution)/shard_map/all_to_all | solution.py:30
  177.9 1.2 copy-start.1
  179.1 21.4 %all-to-all-start.5 = ((bf16[8,1,64,12,128]{4,2,3,1,0:T(8,128)(2,1)}), bf16[8,1,64,12,128]{4,2,3,1,0:T(8,128)(2,1)S(1)}, u32[]{:S(2)}, u32[]{:S(2)}) async-start(bf16[8,1,64,12,128]{4,2,3,1,0:T(8,128)(2,1)} %copy.96), calls=%async_computation.5 | async-start | bytes 3145728 | tf_op jit(solution)/shard_map/all_to_all | solution.py:45
  203.6 46.9 %all-to-all-start.6 = ((bf16[1,64,12,128]{3,2,0,1:T(8,128)(2,1)}), bf16[1,64,12,128]{3,2,0,1:T(8,128)(2,1)}, u32[]{:S(2)}, u32[]{:S(2)}) async-start(bf16[1,64,12,128]{3,2,0,1:T(8,128)(2,1)} %copy.98), calls=%async_computation.6 | async-start | bytes 524288 | tf_op jit(solution)/shard_map/all_to_all | solution.py:99
  250.5 23.7 %all-to-all-start.4 = ((bf16[4,12,128,128]{3,2,1,0:T(8,128)(2,1)}), bf16[4,12,128,128]{3,2,1,0:T(8,128)(2,1)S(1)}, u32[]{:S(2)}, u32[]{:S(2)}) async-start(bf16[4,12,128,128]{3,2,1,0:T(8,128)(2,1)} %bitcast.79), calls=%async_computation.4 | async-start | bytes 3145728 | tf_op jit(solution)/shard_map/all_to_all | solution.py:45
  274.2 44.2 %all-to-all-start.7 = ((bf16[1,4,720,128]{3,1,0,2:T(4,128)(2,1)}), bf16[1,4,720,128]{3,1,0,2:T(4,128)(2,1)}, u32[]{:S(2)}, u32[]{:S(2)}) async-start(bf16[1,4,720,128]{3,1,0,2:T(4,128)(2,1)} %copy.102), calls=%async_computation.7 | async-start | bytes 1474560 | tf_op jit(solution)/shard_map/all_to_all | solution.py:102
where the time goes:
time: 326 us; the launch traced here: 321 us
  waiting for transfers between devices  124 us (38%)
  starting transfers between devices  78 us (24%)
  local copies, waits for them, and re-layouts  64.2 us (20%)
  blocking collectives  29.7 us (9%)
  other arithmetic  15.6 us (5%)
  matrix products  8.85 us (3%)
    all_to_all x1, waiting for transfers between devices, on_device(): lax.all_to_all(grad_output, 'lat', split_axis=1, concat_axis=2, tiled=True)  33.4 us
    all_to_all x1, waiting for transfers between devices, on_device(): lax.all_to_all(saved_input, 'lat', split_axis=1, concat_axis=2, tiled=True)  33.2 us
    all_to_all x1, waiting for transfers between devices, on_device(): lax.all_to_all(grad_local, 'lat', split_axis=2, concat_axis=1, tiled=True)  31.3 us
    all_to_all x1, blocking collectives, side_by_side(): lax.all_to_all(both, axis, split_axis=split_dim, concat_axis=concat_dim,...  29.7 us
    all_to_all x2, waiting for transfers between devices, summed_on_arrival(): lax.all_to_all(pieces, axis, split_axis=0, concat_axis=0, tiled=True)  25.5 us
    all_to_all x1, starting transfers between devices, on_device(): lax.all_to_all(grad_spec_in, 'lat', split_axis=1, concat_axis=2, tiled=True)  20.5 us
    unnamed x17, local copies, waits for them, and re-layouts  19.6 us
    all_to_all x1, starting transfers between devices, on_device(): lax.all_to_all(saved_input, 'lat', split_axis=1, concat_axis=2, tiled=True)  15.7 us
  transfers between devices with their start and end apart: 7, of which 5 were waited for; matrix products, arithmetic and copies ran while one was open for 23% of the time, Pallas kernels for 0%

commit v1 on v0

v1 whole, which is shorter than its diff:
```python
import jax
import jax.numpy as jnp
from jax import lax
from jax.experimental import pallas as pl
from jax.experimental.pallas import tpu as pltpu
from jax.sharding import PartitionSpec as P

MESH = pl.DeviceIdType.MESH
BF = jnp.bfloat16
F32 = jnp.float32

M, J, Q, LB, MB, CH, NZ = 64, 45, 128, 12, 4, 192, 16
ROWS = NZ * LB * MB
NCHAN, NDP = 8, 4


def iota(shape, dim):
    return lax.broadcasted_iota(jnp.int32, shape, dim)


def dot(a, b, dims=((1,), (0,))):
    return lax.dot_general(a, b, (dims, ((), ())), preferred_element_type=F32)


def one_hot(hit):
    return jnp.where(hit, 1.0, 0.0).astype(BF)


def offset_of(s):
    k = (s + 1) // 2
    far = 8 - k
    return jnp.where(s % 2 == 1, far, NZ - far)


def kernel(
    go, si, leg, quad, w, gw, gi,
    r_syn, r_ana, t_syn, t_ana, t_back, p_in, p_out, p_sort, p_unsort, w2,
    g1s, g1r, s1s, s1r, acc, g2s, g2r, s2s, s2r, gall, sall, ks, kr, b3s, b3r, o4s, o4r,
    g_ss, g_rs, s_ss, s_rs, g2_ss, g2_rs, s2_ss, s2_rs, k_ss, k_rs, d_ss, d_rs, e_ss, e_rs,
    b_ss, b_rs, o_ss, o_rs,
):
    dp, z, ch = lax.axis_index("dp"), lax.axis_index("lat"), lax.axis_index("chan")
    barrier = pltpu.get_barrier_semaphore()

    def greet_z(s, c):
        to = (z + s + 1) % NZ
        pl.semaphore_signal(barrier, inc=1, device_id={"lat": to}, device_id_type=MESH)
        return c

    def greet_plane(s, c):
        other = (dp * NCHAN + ch + s + 1) % (NDP * NCHAN)
        pl.semaphore_signal(
            barrier, inc=1, device_id={"dp": other // NCHAN, "chan": other % NCHAN}, device_id_type=MESH
        )
        return c

    lax.fori_loop(0, NZ - 1, greet_z, 0)
    lax.fori_loop(0, NDP * NCHAN - 1, greet_plane, 0)

    def z_copy(src, dst, ss, rs, to, slot):
        return pltpu.make_async_remote_copy(
            src_ref=src.at[to], dst_ref=dst.at[slot], send_sem=ss.at[to], recv_sem=rs.at[slot],
            device_id={"lat": to}, device_id_type=MESH,
        )

    def z_send(src, dst, ss, rs, first, last, flip=False):
        def step(s, c):
            to = (z + offset_of(NZ - 2 - s if flip else s)) % NZ
            z_copy(src, dst, ss, rs, to, z).start()
            return c

        lax.fori_loop(first, last, step, 0)

    def z_wait_sends(src, dst, ss, rs):
        def step(s, c):
            z_copy(src, dst, ss, rs, (z + s + 1) % NZ, z).wait_send()
            return c

        lax.fori_loop(0, NZ - 1, step, 0)

    def z_wait_recv(src, dst, ss, rs, s):
        frm = (z + NZ - offset_of(s)) % NZ
        z_copy(src, dst, ss, rs, frm, frm).wait_recv()
        return frm

    def z_wait_all(src, dst, ss, rs):
        def step(s, c):
            z_wait_recv(src, dst, ss, rs, s)
            return c

        lax.fori_loop(0, NZ - 1, step, 0)

    for zz in range(4):
        r, c = iota((CH, 16 * J), 0), iota((CH, 16 * J), 1)
        p_in[pl.ds(zz * CH, CH), :] = one_hot((c == (r // 4) * 16 + zz * 4 + r % 4) & (r < MB * J))

    def order_in(x, out):
        def step(g, c):
            rows = x[:, pl.ds(pl.multiple_of(16 * g, 16), 16), :].reshape(16 * J, Q)
            out[pl.ds(4 * g, 4)] = dot(p_in[...], rows).astype(BF).reshape(4, CH, Q)
            return c

        lax.fori_loop(0, 4, step, 0)

    order_in(go, g1s)
    pl.semaphore_wait(barrier, NZ - 1 + NDP * NCHAN - 1)
    z_send(g1s, g1r, g_ss, g_rs, 0, NZ - 1)
    order_in(si, s1s)
    z_send(s1s, s1r, s_ss, s_rs, 0, 8, flip=True)
    g1r[z] = g1s[z]
    s1r[z] = s1s[z]

    zero = jnp.zeros((ROWS, ROWS - 720), BF)
    r_syn[:, 720:] = zero
    r_ana[:, 720:] = zero

    def rows_of(ib, c):
        r = iota((128, ROWS), 0) + ib * 128
        pick = one_hot(iota((128, ROWS), 1) == (r % 4) * (NZ * LB) + r // 4)
        flat = leg[...].reshape(ROWS, 720)
        at = pl.ds(pl.multiple_of(ib * 128, 128), 128)
        syn = dot(pick, flat)
        r_syn[at, :720] = syn.astype(BF)
        r_ana[at, :720] = (syn * quad[...]).astype(BF)
        return c

    lax.fori_loop(0, ROWS // 128, rows_of, 0)

    def window(zz):
        start = jnp.minimum((zz * J) // 128, 4) * 128
        return pl.ds(pl.multiple_of(start, 128), 256), zz * J - start

    def table(src, dst):
        def step(zz, c):
            at, off = window(zz)
            r, k = iota((256, CH), 0), iota((256, CH), 1)
            pick = one_hot((r == off + k // 4) & (k < MB * J))
            full = dot(src[:, at], pick)
            keep = iota((ROWS, CH), 0) % 4 == iota((ROWS, CH), 1) % 4
            dst[zz] = jnp.where(keep, full, 0.0).astype(BF)
            return c

        lax.fori_loop(0, NZ, step, 0)

    table(r_syn, t_syn)

    def sort_block(ib, c):
        at = pl.ds(pl.multiple_of(ib * 128, 128), 128)
        r, k = iota((128, ROWS), 0) + ib * 128, iota((128, ROWS), 1)
        p_sort[at, :] = one_hot(k == ((r % M) // 4) * 48 + (r // M) * 4 + r % 4)
        p_unsort[at, :] = one_hot(r == ((k % M) // 4) * 48 + (k // M) * 4 + k % 4)
        return c

    lax.fori_loop(0, ROWS // 128, sort_block, 0)

    ra, ca = iota((Q, Q), 0), iota((Q, Q), 1)
    swap = jnp.where(ca == ra + 1, 1.0, 0.0) * jnp.where(ra % 2 == 0, 1.0, 0.0)
    swap = (swap - jnp.where(ra == ca + 1, 1.0, 0.0) * jnp.where(ca % 2 == 0, 1.0, 0.0)).astype(BF)
    r2, c2 = iota((256, 256), 0), iota((256, 256), 1)
    weave = one_hot(c2 == (r2 % 2) * 128 + r2 // 2)

    def weave_weight(l, c):
        for k in range(4):
            block = w[l, pl.ds(128 * k, 128), :]
            both = jnp.concatenate([block, dot(block, swap).astype(BF)], axis=0)
            w2[l, pl.ds(256 * k, 256), :] = dot(weave, both).astype(BF)
        return c

    lax.fori_loop(0, LB, weave_weight, 0)
    table(r_ana, t_ana)

    def back_table(zz, c):
        at, off = window(zz)
        r, k = iota((CH, 256), 0), iota((CH, 256), 1)
        pick = one_hot((k == off + r // 4) & (r < MB * J))
        full = dot(pick, r_ana[:, at], ((1,), (1,)))
        keep = iota((CH, ROWS), 0) % 4 == iota((CH, ROWS), 1) % 4
        t_back[zz] = jnp.where(keep, full, 0.0).astype(BF)
        return c

    lax.fori_loop(0, NZ, back_table, 0)

    def legendre_sum(t, send, recv, ss, rs, out, flip=False):
        acc[...] = dot(t[z], recv[z])

        def step(s, c):
            frm = z_wait_recv(send, recv, ss, rs, NZ - 2 - s if flip else s)
            acc[...] += dot(t[frm], recv[frm])
            return c

        lax.fori_loop(0, NZ - 1, step, 0)
        out[...] = acc[...].astype(BF).reshape(NZ, LB * MB, Q)

    legendre_sum(t_syn, g1s, g1r, g_ss, g_rs, g2s)
    z_send(g2s, g2r, g2_ss, g2_rs, 0, NZ - 1)
    z_send(s1s, s1r, s_ss, s_rs, 8, NZ - 1, flip=True)
    g2r[z] = g2s[z]
    z_wait_all(g2s, g2r, g2_ss, g2_rs)
    grads = dot(p_sort[...], g2r[...].reshape(ROWS, Q)).astype(BF).reshape(LB, M, Q)
    gall[dp] = grads

    def mix(l, c):
        full = dot(gall[dp, l], w2[l], ((1,), (1,))).astype(BF)
        for k in range(NCHAN):
            ks[k, l] = full[:, 128 * k : 128 * k + 128]
        return c

    lax.fori_loop(0, LB, mix, 0)

    def k_copy(to, slot):
        return pltpu.make_async_remote_copy(
            src_ref=ks.at[to], dst_ref=kr.at[slot], send_sem=k_ss.at[to], recv_sem=k_rs.at[slot],
            device_id={"chan": to}, device_id_type=MESH,
        )

    def k_send(s, c):
        k_copy((ch + s + 1) % NCHAN, ch).start()
        return c

    lax.fori_loop(0, NCHAN - 1, k_send, 0)

    def d_copy(to, slot):
        return pltpu.make_async_remote_copy(
            src_ref=gall.at[dp], dst_ref=gall.at[slot], send_sem=d_ss.at[to], recv_sem=d_rs.at[slot],
            device_id={"dp": to}, device_id_type=MESH,
        )

    def d_send(s, c):
        d_copy((dp + s + 1) % NDP, dp).start()
        return c

    lax.fori_loop(0, NDP - 1, d_send, 0)
    kr[ch] = ks[ch]

    legendre_sum(t_ana, s1s, s1r, s_ss, s_rs, s2s, flip=True)
    z_send(s2s, s2r, s2_ss, s2_rs, 0, NZ - 1)
    s2r[z] = s2s[z]

    def k_wait(s, c):
        frm = (ch + s + 1) % NCHAN
        k_copy(frm, frm).wait_recv()
        return c

    lax.fori_loop(0, NCHAN - 1, k_wait, 0)

    def sum_terms(l, c):
        total = kr[0, l].astype(F32)
        for k in range(1, NCHAN):
            total = total + kr[k, l].astype(F32)
        kr[0, l] = total.astype(BF)
        return c

    lax.fori_loop(0, LB, sum_terms, 0)
    b3s[...] = dot(p_unsort[...], kr[0].reshape(ROWS, Q)).astype(BF).reshape(NZ, LB * MB, Q)
    z_send(b3s, b3r, b_ss, b_rs, 0, NZ - 1)
    b3r[z] = b3s[z]

    home, half = ch // 2, ch % 2
    z_wait_all(s2s, s2r, s2_ss, s2_rs)
    mine = sall.at[dp, half]
    spectra = dot(p_sort[...], s2r[...].reshape(ROWS, Q)).astype(BF).reshape(LB, M, Q)
    s2all = ks.at[ch]
    s2all[...] = spectra

    def e_copy(to, b, h):
        return pltpu.make_async_remote_copy(
            src_ref=ks.at[ch], dst_ref=sall.at[b, h], send_sem=e_ss.at[to], recv_sem=e_rs.at[b, h],
            device_id={"dp": home, "chan": to}, device_id_type=MESH,
        )

    def e_send(s, c):
        to = (ch + s) % NCHAN

        @pl.when((to != ch) | (home != dp))
        def _():
            e_copy(to, dp, half).start()

        return c

    lax.fori_loop(0, NCHAN, e_send, 0)

    @pl.when(home == dp)
    def _():
        mine[...] = spectra

    z_wait_all(b3s, b3r, b_ss, b_rs)

    def back(s, c):
        to = (z + offset_of(s)) % NZ
        o4s[to] = dot(t_back[to], b3r[...].reshape(ROWS, Q)).astype(BF)
        z_copy(o4s, o4r, o_ss, o_rs, to, z).start()
        return c

    lax.fori_loop(0, NZ - 1, back, 0)
    o4r[z] = dot(t_back[z], b3r[...].reshape(ROWS, Q)).astype(BF)
    for zz in range(4):
        r, c = iota((16 * J, CH), 0), iota((16 * J, CH), 1)
        p_out[:, pl.ds(zz * CH, CH)] = one_hot((r == (c // 4) * 16 + zz * 4 + c % 4) & (c < MB * J))

    def d_wait(s, c):
        frm = (dp + s + 1) % NDP
        d_copy(frm, frm).wait_recv()
        return c

    lax.fori_loop(0, NDP - 1, d_wait, 0)
    for b in range(NDP):
        for h in range(2):

            @pl.when((b != dp) | (2 * dp + h != ch))
            def _():
                e_copy(ch, b, h).wait_recv()

    apart = one_hot(r2 == 2 * (c2 % 128) + c2 // 128)
    partner_of = (-swap.astype(F32)).astype(BF)

    def weight(l, c):
        left, right = [], []
        for b in range(NDP):
            both = jnp.concatenate([sall[b, 0, l], sall[b, 1, l]], axis=1)
            parts = dot(both, apart).astype(BF)
            left += [parts[:, :128], parts[:, 128:]]
            g = gall[b, l]
            right += [g, dot(g, partner_of).astype(BF)]
        total = dot(jnp.concatenate(left, axis=0), jnp.concatenate(right, axis=0), ((0,), (0,)))
        gw[l] = (total * 0.25).astype(BF)
        return c

    lax.fori_loop(0, LB, weight, 0)

    z_wait_all(o4s, o4r, o_ss, o_rs)

    def order_out(g, c):
        rows = o4r[pl.ds(4 * g, 4)].reshape(4 * CH, Q)
        out = dot(p_out[...], rows).astype(BF).reshape(J, 16, Q)
        gi[:, pl.ds(pl.multiple_of(16 * g, 16), 16), :] = out
        return c

    lax.fori_loop(0, 4, order_out, 0)

    for args in (
        (g1s, g1r, g_ss, g_rs), (s1s, s1r, s_ss, s_rs), (g2s, g2r, g2_ss, g2_rs),
        (s2s, s2r, s2_ss, s2_rs), (b3s, b3r, b_ss, b_rs), (o4s, o4r, o_ss, o_rs),
    ):
        z_wait_sends(*args)

    def k_done(s, c):
        k_copy((ch + s + 1) % NCHAN, ch).wait_send()
        return c

    lax.fori_loop(0, NCHAN - 1, k_done, 0)

    def d_done(s, c):
        d_copy((dp + s + 1) % NDP, dp).wait_send()
        return c

    lax.fori_loop(0, NDP - 1, d_done, 0)

    def e_done(s, c):
        to = (ch + s) % NCHAN

        @pl.when((to != ch) | (home != dp))
        def _():
            e_copy(to, dp, half).wait_send()

        return c

    lax.fori_loop(0, NCHAN, e_done, 0)


def on_device(saved_input, grad_output, legendre, quad_weight, mixing_weight):
    go = grad_output[0].transpose(1, 0, 2)
    si = saved_input[0].transpose(1, 0, 2)
    vmem = pl.BlockSpec(memory_space=pltpu.VMEM)
    dma = pltpu.SemaphoreType.DMA
    gw, gi = pl.pallas_call(
        kernel,
        out_shape=(
            jax.ShapeDtypeStruct((LB, Q, Q), BF),
            jax.ShapeDtypeStruct((J, M, Q), BF),
        ),
        in_specs=[vmem] * 5,
        out_specs=(vmem, vmem),
        scratch_shapes=[
            pltpu.VMEM((ROWS, ROWS), BF), pltpu.VMEM((ROWS, ROWS), BF),
            pltpu.VMEM((NZ, ROWS, CH), BF), pltpu.VMEM((NZ, ROWS, CH), BF),
            pltpu.VMEM((NZ, CH, ROWS), BF),
            pltpu.VMEM((4 * CH, 16 * J), BF), pltpu.VMEM((16 * J, 4 * CH), BF),
            pltpu.VMEM((ROWS, ROWS), BF), pltpu.VMEM((ROWS, ROWS), BF),
            pltpu.VMEM((LB, 1024, Q), BF),
            pltpu.VMEM((NZ, CH, Q), BF), pltpu.VMEM((NZ, CH, Q), BF),
            pltpu.VMEM((NZ, CH, Q), BF), pltpu.VMEM((NZ, CH, Q), BF),
            pltpu.VMEM((ROWS, Q), F32),
            pltpu.VMEM((NZ, LB * MB, Q), BF), pltpu.VMEM((NZ, LB * MB, Q), BF),
            pltpu.VMEM((NZ, LB * MB, Q), BF), pltpu.VMEM((NZ, LB * MB, Q), BF),
            pltpu.VMEM((NDP, LB, M, Q), BF), pltpu.VMEM((NDP, 2, LB, M, Q), BF),
            pltpu.VMEM((NCHAN, LB, M, Q), BF), pltpu.VMEM((NCHAN, LB, M, Q), BF),
            pltpu.VMEM((NZ, LB * MB, Q), BF), pltpu.VMEM((NZ, LB * MB, Q), BF),
            pltpu.VMEM((NZ, CH, Q), BF), pltpu.VMEM((NZ, CH, Q), BF),
            dma((NZ,)), dma((NZ,)), dma((NZ,)), dma((NZ,)), dma((NZ,)), dma((NZ,)),
            dma((NZ,)), dma((NZ,)), dma((NCHAN,)), dma((NCHAN,)), dma((NDP,)), dma((NDP,)),
            dma((NCHAN,)), dma((NDP, 2)), dma((NZ,)), dma((NZ,)), dma((NZ,)), dma((NZ,)),
        ],
        compiler_params=pltpu.CompilerParams(
            collective_id=0, has_side_effects=True, vmem_limit_bytes=63_000_000
        ),
    )(go, si, legendre, quad_weight[None, :], mixing_weight)
    return gw, gi.transpose(1, 0, 2)[None]


def solution(mesh):
    in_specs = (
        P("dp", None, "lat", "chan"),
        P("dp", None, "lat", "chan"),
        P("lat", None, None),
        P(),
        P("lat", None, "chan"),
    )
    out_specs = (P("lat", "dp", "chan"), P("dp", None, "lat", "chan"))
    return jax.shard_map(
        on_device, mesh=mesh, in_specs=in_specs, out_specs=out_specs, check_vma=False
    )
```

time: 326 us -> 165 us (0.51); the launches traced: 321 us -> 164 us
  Pallas kernels: 0 us -> 159 us
  waiting for transfers between devices: 124 us -> 0 us
  starting transfers between devices: 78 us -> 0 us
  local copies, waits for them, and re-layouts: 64.2 us -> 5.06 us
  blocking collectives: 29.7 us -> 0 us
  other arithmetic: 15.6 us -> 0 us
  matrix products: 8.85 us -> 0 us
    pallas_call x0 -> x1, Pallas kernels: none -> 159 us  [on_device(): pl.pallas_call(kernel, out_shape=(jax.ShapeDtypeStruct((LB, Q, Q), BF), j...]
    all_to_all x7 -> x0, waiting for transfers between devices: 124 us -> none  [the longest x1 33.4 us: on_device(): lax.all_to_all(grad_output, 'lat', split_axis=1, concat_axis=2, tiled=True)]
    all_to_all x7 -> x0, starting transfers between devices: 78 us -> none  [the longest x1 20.5 us: on_device(): lax.all_to_all(grad_spec_in, 'lat', split_axis=1, concat_axis=2, tiled=True)]
    all_to_all x1 -> x0, blocking collectives: 29.7 us -> none  [side_by_side(): lax.all_to_all(both, axis, split_axis=split_dim, concat_axis=concat_dim,...]
    unnamed x17 -> x2, local copies, waits for them, and re-layouts: 19.6 us -> 3.79 us
    another operation x2 -> x0, local copies, waits for them, and re-layouts: 13.5 us -> none  [the longest x1 8.35 us: on_device(): terms = jnp.stack([sum_real, sum_imag], axis=-1)]
    slice x1 -> x0, local copies, waits for them, and re-layouts: 9.55 us -> none  [weight_terms(): pairs[..., 1]]
    dot_general x7 -> x0, matrix products: 8.85 us -> none  [the longest x1 1.97 us: on_device(): jnp.einsum('mlj,bmlq->bmjq', analysis, lax.all_to_all(grad_spec_in, 'lat'...]
  transfers between devices with their start and end apart: 7 -> 0, of which waited for: 5 -> 0; matrix products, arithmetic and copies ran while one was open for 23% -> 0% of each run, Pallas kernels for 0% -> 0%
where the time goes in v1:
time: 165 us; the launch traced here: 164 us
  Pallas kernels  159 us (96%)
  local copies, waits for them, and re-layouts  5.06 us (3%)
    pallas_call x1, Pallas kernels, on_device(): pl.pallas_call(kernel, out_shape=(jax.ShapeDtypeStruct((LB, Q, Q), BF), j...  159 us
    unnamed x2, local copies, waits for them, and re-layouts  3.79 us

profile of v1, /device:TPU:1, one launch (start us, length us, event | category | flops | bytes accessed | tf_op | source)
XLA Modules:
  0.0 164.5 jit_solution(17019212197318119156)
XLA Ops:
  0.6 1.3 broadcast_in_dim.6.quad
  1.9 158.8 %shard_map.68 = (bf16[12,128,128]{2,1,0:T(8,128)(2,1)}, bf16[45,64,128]{2,1,0:T(8,128)(2,1)}) custom-call(bf16[45,64,128]{2,1,0:T(8,128)(2,1)} %bitcast.9, bf16[45,64,128]{2,1,0:T(8,128)(2,1)} %bitcast.10, bf16[4,192,720]{2,1,0:T(8,128)(2,1)} %leg.1, f32[1,720]{1,0:T(1,128)} %broadcast_in_dim.6.quad, bf16[12,512,128]{2,1,0:T(8,128)(2,1)} %w.1), custom_call_target="tpu_custom_call" | custom-call | tf_op jit(solution)/shard_map/pallas_call | solution.py:375
  160.7 1.8 %copy.9 = bf16[12,128,128]{2,1,0:T(8,128)(2,1)} copy(bf16[12,128,128]{2,1,0:T(8,128)(2,1)} %get-tuple-element.8) | data formatting | bytes 786432
  162.4 2.0 %copy.10 = bf16[1,64,45,128]{3,1,2,0:T(8,128)(2,1)} copy(bf16[1,64,45,128]{3,1,2,0:T(8,128)(2,1)} %bitcast.11) | data formatting | bytes 1474560

commit v2 on v1

--- a/solution.py
+++ b/solution.py
@@ -12,6 +12,7 @@
 M, J, Q, LB, MB, CH, NZ = 64, 45, 128, 12, 4, 192, 16
 ROWS = NZ * LB * MB
 NCHAN, NDP = 8, 4
+SHARES = 24
 
 
 def iota(shape, dim):
@@ -34,10 +35,11 @@
 
 def kernel(
     go, si, leg, quad, w, gw, gi,
-    r_syn, r_ana, t_syn, t_ana, t_back, p_in, p_out, p_sort, p_unsort, w2,
-    g1s, g1r, s1s, s1r, acc, g2s, g2r, s2s, s2r, gall, sall, ks, kr, b3s, b3r, o4s, o4r,
+    r_syn, r_ana, t_syn, t_ana, p_in, p_sort, p_unsort, w2,
+    g1s, g1r, s1s, s1r, acc, g2s, g2r, s2s, s2r, gall, sall, ks, kr,
+    xa, tsend, trecv, tall, xr, t_back, ag, oacc,
     g_ss, g_rs, s_ss, s_rs, g2_ss, g2_rs, s2_ss, s2_rs, k_ss, k_rs, d_ss, d_rs, e_ss, e_rs,
-    b_ss, b_rs, o_ss, o_rs,
+    t_ss, t_rs, a_ss, a_rs, r_ss, r_rs,
 ):
     dp, z, ch = lax.axis_index("dp"), lax.axis_index("lat"), lax.axis_index("chan")
     barrier = pltpu.get_barrier_semaphore()
@@ -104,7 +106,36 @@
 
     order_in(go, g1s)
     pl.semaphore_wait(barrier, NZ - 1 + NDP * NCHAN - 1)
-    z_send(g1s, g1r, g_ss, g_rs, 0, NZ - 1)
+    z_send(g1s, g1r, g_ss, g_rs, 0, 3)
+
+    me = dp * NCHAN + ch
+    shares = me < SHARES
+    group, pair = jnp.minimum(me // 2, SHARES // 2 - 1), me % 2
+    for h in range(2):
+        part = leg[2 * pair + h, pl.ds(pl.multiple_of(16 * group, 16), 16), :].astype(F32)
+        xa[h, :, 720:] = jnp.zeros((16, ROWS - 720), BF)
+        xa[h, :, :720] = (part * quad[...]).astype(BF)
+
+    def window(zz):
+        start = jnp.minimum((zz * J) // 128, 4) * 128
+        return pl.ds(pl.multiple_of(start, 128), 256), zz * J - start
+
+    def cut(zz, c):
+        at, off = window(zz)
+        r, k = iota((512, 128), 0), iota((512, 128), 1)
+        pick = one_hot((r % 256 == off + k % 64) & (r // 256 == k // 64) & (k % 64 < J))
+        both = jnp.concatenate([xa[0, :, at], xa[1, :, at]], axis=1)
+        tsend[zz] = dot(both, pick).astype(BF)
+        return c
+
+    lax.fori_loop(0, NZ, cut, 0)
+
+    @pl.when(shares)
+    def _():
+        z_send(tsend, trecv, t_ss, t_rs, 0, NZ - 1)
+
+    trecv[z] = tsend[z]
+    z_send(g1s, g1r, g_ss, g_rs, 3, NZ - 1)
     order_in(si, s1s)
     z_send(s1s, s1r, s_ss, s_rs, 0, 8, flip=True)
     g1r[z] = g1s[z]
@@ -126,10 +157,6 @@
 
     lax.fori_loop(0, ROWS // 128, rows_of, 0)
 
-    def window(zz):
-        start = jnp.minimum((zz * J) // 128, 4) * 128
-        return pl.ds(pl.multiple_of(start, 128), 256), zz * J - start
-
     def table(src, dst):
         def step(zz, c):
             at, off = window(zz)
@@ -148,7 +175,7 @@
         at = pl.ds(pl.multiple_of(ib * 128, 128), 128)
         r, k = iota((128, ROWS), 0) + ib * 128, iota((128, ROWS), 1)
         p_sort[at, :] = one_hot(k == ((r % M) // 4) * 48 + (r // M) * 4 + r % 4)
-        p_unsort[at, :] = one_hot(r == ((k % M) // 4) * 48 + (k // M) * 4 + k % 4)
+        p_unsort[at, :] = one_hot(k == ((r % 96) // 8) * M + (r // 96) * 8 + r % 8)
         return c
 
     lax.fori_loop(0, ROWS // 128, sort_block, 0)
@@ -167,18 +194,25 @@
         return c
 
     lax.fori_loop(0, LB, weave_weight, 0)
+
+    def a_copy(to, frm):
+        return pltpu.make_async_remote_copy(
+            src_ref=trecv, dst_ref=tall.at[frm], send_sem=a_ss.at[to], recv_sem=a_rs.at[frm],
+            device_id={"dp": to // NCHAN, "chan": to % NCHAN}, device_id_type=MESH,
+        )
+
+    @pl.when(shares)
+    def _():
+        z_wait_all(tsend, trecv, t_ss, t_rs)
+
+        def a_send(s, c):
+            a_copy((me + s + 1) % (NDP * NCHAN), me).start()
+            return c
+
+        lax.fori_loop(0, NDP * NCHAN - 1, a_send, 0)
+        tall[me] = trecv[...]
+
     table(r_ana, t_ana)
-
-    def back_table(zz, c):
-        at, off = window(zz)
-        r, k = iota((CH, 256), 0), iota((CH, 256), 1)
-        pick = one_hot((k == off + r // 4) & (r < MB * J))
-        full = dot(pick, r_ana[:, at], ((1,), (1,)))
-        keep = iota((CH, ROWS), 0) % 4 == iota((CH, ROWS), 1) % 4
-        t_back[zz] = jnp.where(keep, full, 0.0).astype(BF)
-        return c
-
-    lax.fori_loop(0, NZ, back_table, 0)
 
     def legendre_sum(t, send, recv, ss, rs, out, flip=False):
         acc[...] = dot(t[z], recv[z])
@@ -232,6 +266,37 @@
     lax.fori_loop(0, NDP - 1, d_send, 0)
     kr[ch] = ks[ch]
 
+    def a_wait(s, c):
+        @pl.when(s != me)
+        def _():
+            a_copy(s, s).wait_recv()
+
+        return c
+
+    lax.fori_loop(0, SHARES, a_wait, 0)
+    rx, cx = iota((128, 64), 0), iota((128, 64), 1)
+    spread = one_hot(cx == ((rx % 8) // 2) * 16 + rx // 8)
+
+    def by_degree(i, c):
+        g, lg = i % 8, i // 8
+        tiles = [tall[2 * lg + t % 2, 2 * g + t // 2] for t in range(4)]
+        at = pl.ds(pl.multiple_of(lg * 128, 128), 128)
+        xr[g, at, :] = dot(spread, jnp.concatenate(tiles, axis=0)).astype(BF)
+        return c
+
+    lax.fori_loop(0, 96, by_degree, 0)
+
+    def back_table(i, c):
+        g, o = i % 8, i // 8
+        r, k = iota((8 * J, 128), 0), iota((8 * J, 128), 1)
+        pick = one_hot(k == (r % 2) * 64 + r // 8)
+        full = dot(pick, xr[g, pl.ds(pl.multiple_of(o * 96, 32), 96), :], ((1,), (1,)))
+        keep = iota((8 * J, 96), 0) % 8 == iota((8 * J, 96), 1) % 8
+        t_back[o, g] = jnp.where(keep, full, 0.0).astype(BF)
+        return c
+
+    lax.fori_loop(0, 8 * NZ, back_table, 0)
+
     legendre_sum(t_ana, s1s, s1r, s_ss, s_rs, s2s, flip=True)
     z_send(s2s, s2r, s2_ss, s2_rs, 0, NZ - 1)
     s2r[z] = s2s[z]
@@ -251,9 +316,20 @@
         return c
 
     lax.fori_loop(0, LB, sum_terms, 0)
-    b3s[...] = dot(p_unsort[...], kr[0].reshape(ROWS, Q)).astype(BF).reshape(NZ, LB * MB, Q)
-    z_send(b3s, b3r, b_ss, b_rs, 0, NZ - 1)
-    b3r[z] = b3s[z]
+    ag[z] = dot(p_unsort[...], kr[0].reshape(ROWS, Q)).astype(BF).reshape(8, 96, Q)
+
+    def r_copy(side, hop, part, origin):
+        to = (z + (1 if side == 0 else NZ - 1)) % NZ
+        at = pl.ds(2 * part, 2)
+        return pltpu.make_async_remote_copy(
+            src_ref=ag.at[origin, at], dst_ref=ag.at[origin, at],
+            send_sem=r_ss.at[side, hop, part], recv_sem=r_rs.at[side, hop, part],
+            device_id={"lat": to}, device_id_type=MESH,
+        )
+
+    for part in range(4):
+        for side in range(2):
+            r_copy(side, 0, part, z).start()
 
     home, half = ch // 2, ch % 2
     z_wait_all(s2s, s2r, s2_ss, s2_rs)
@@ -283,19 +359,27 @@
     def _():
         mine[...] = spectra
 
-    z_wait_all(b3s, b3r, b_ss, b_rs)
-
-    def back(s, c):
-        to = (z + offset_of(s)) % NZ
-        o4s[to] = dot(t_back[to], b3r[...].reshape(ROWS, Q)).astype(BF)
-        z_copy(o4s, o4r, o_ss, o_rs, to, z).start()
-        return c
-
-    lax.fori_loop(0, NZ - 1, back, 0)
-    o4r[z] = dot(t_back[z], b3r[...].reshape(ROWS, Q)).astype(BF)
-    for zz in range(4):
-        r, c = iota((16 * J, CH), 0), iota((16 * J, CH), 1)
-        p_out[:, pl.ds(zz * CH, CH)] = one_hot((r == (c // 4) * 16 + zz * 4 + c % 4) & (c < MB * J))
+    for g in range(8):
+        oacc[g] = dot(t_back[z, g], ag[z, g])
+
+    def hop_in(k, c):
+        left, right = (z + NZ - k) % NZ, (z + k) % NZ
+        for part in range(4):
+            for side, origin in ((0, left), (1, right)):
+                r_copy(side, k - 1, part, origin).wait_recv()
+                if part // 2 == side:
+                    r_copy(side, k, part, origin).start()
+                else:
+
+                    @pl.when(k < NZ // 2 - 1)
+                    def _():
+                        r_copy(side, k, part, origin).start()
+
+            for g in (2 * part, 2 * part + 1):
+                oacc[g] += dot(t_back[left, g], ag[left, g]) + dot(t_back[right, g], ag[right, g])
+        return c
+
+    lax.fori_loop(1, NZ // 2, hop_in, 0)
 
     def d_wait(s, c):
         frm = (dp + s + 1) % NDP
@@ -327,21 +411,39 @@
 
     lax.fori_loop(0, LB, weight, 0)
 
-    z_wait_all(o4s, o4r, o_ss, o_rs)
-
-    def order_out(g, c):
-        rows = o4r[pl.ds(4 * g, 4)].reshape(4 * CH, Q)
-        out = dot(p_out[...], rows).astype(BF).reshape(J, 16, Q)
-        gi[:, pl.ds(pl.multiple_of(16 * g, 16), 16), :] = out
-        return c
-
-    lax.fori_loop(0, 4, order_out, 0)
+    across = (z + NZ // 2) % NZ
+    for part in range(4):
+        r_copy(part // 2, NZ // 2 - 1, part, across).wait_recv()
+        halves = []
+        for g in (2 * part, 2 * part + 1):
+            halves.append((oacc[g] + dot(t_back[across, g], ag[across, g])).reshape(J, 8, Q))
+        gi[:, pl.ds(16 * part, 16), :] = jnp.concatenate(halves, axis=1).astype(BF)
 
     for args in (
         (g1s, g1r, g_ss, g_rs), (s1s, s1r, s_ss, s_rs), (g2s, g2r, g2_ss, g2_rs),
-        (s2s, s2r, s2_ss, s2_rs), (b3s, b3r, b_ss, b_rs), (o4s, o4r, o_ss, o_rs),
+        (s2s, s2r, s2_ss, s2_rs),
     ):
         z_wait_sends(*args)
+
+    @pl.when(shares)
+    def _():
+        z_wait_sends(tsend, trecv, t_ss, t_rs)
+
+        def a_done(s, c):
+            a_copy((me + s + 1) % (NDP * NCHAN), me).wait_send()
+            return c
+
+        lax.fori_loop(0, NDP * NCHAN - 1, a_done, 0)
+
+    def r_done(k, c):
+        for part in range(4):
+            for side in range(2):
+                r_copy(side, k, part, z).wait_send()
+        return c
+
+    lax.fori_loop(0, NZ // 2 - 1, r_done, 0)
+    for part in range(4):
+        r_copy(part // 2, NZ // 2 - 1, part, z).wait_send()
 
     def k_done(s, c):
         k_copy((ch + s + 1) % NCHAN, ch).wait_send()
@@ -383,8 +485,7 @@
         scratch_shapes=[
             pltpu.VMEM((ROWS, ROWS), BF), pltpu.VMEM((ROWS, ROWS), BF),
             pltpu.VMEM((NZ, ROWS, CH), BF), pltpu.VMEM((NZ, ROWS, CH), BF),
-            pltpu.VMEM((NZ, CH, ROWS), BF),
-            pltpu.VMEM((4 * CH, 16 * J), BF), pltpu.VMEM((16 * J, 4 * CH), BF),
+            pltpu.VMEM((4 * CH, 16 * J), BF),
             pltpu.VMEM((ROWS, ROWS), BF), pltpu.VMEM((ROWS, ROWS), BF),
             pltpu.VMEM((LB, 1024, Q), BF),
             pltpu.VMEM((NZ, CH, Q), BF), pltpu.VMEM((NZ, CH, Q), BF),
@@ -394,11 +495,14 @@
             pltpu.VMEM((NZ, LB * MB, Q), BF), pltpu.VMEM((NZ, LB * MB, Q), BF),
             pltpu.VMEM((NDP, LB, M, Q), BF), pltpu.VMEM((NDP, 2, LB, M, Q), BF),
             pltpu.VMEM((NCHAN, LB, M, Q), BF), pltpu.VMEM((NCHAN, LB, M, Q), BF),
-            pltpu.VMEM((NZ, LB * MB, Q), BF), pltpu.VMEM((NZ, LB * MB, Q), BF),
-            pltpu.VMEM((NZ, CH, Q), BF), pltpu.VMEM((NZ, CH, Q), BF),
+            pltpu.VMEM((2, 16, ROWS), BF), pltpu.VMEM((NZ, 16, 128), BF), pltpu.VMEM((NZ, 16, 128), BF),
+            pltpu.VMEM((SHARES, NZ, 16, 128), BF), pltpu.VMEM((8, 8 * CH, 128), BF),
+            pltpu.VMEM((NZ, 8, 8 * J, 96), BF), pltpu.VMEM((NZ, 8, 96, Q), BF),
+            pltpu.VMEM((8, 8 * J, Q), F32),
             dma((NZ,)), dma((NZ,)), dma((NZ,)), dma((NZ,)), dma((NZ,)), dma((NZ,)),
             dma((NZ,)), dma((NZ,)), dma((NCHAN,)), dma((NCHAN,)), dma((NDP,)), dma((NDP,)),
-            dma((NCHAN,)), dma((NDP, 2)), dma((NZ,)), dma((NZ,)), dma((NZ,)), dma((NZ,)),
+            dma((NCHAN,)), dma((NDP, 2)), dma((NZ,)), dma((NZ,)),
+            dma((NDP * NCHAN,)), dma((SHARES,)), dma((2, NZ // 2, 4)), dma((2, NZ // 2, 4)),
         ],
         compiler_params=pltpu.CompilerParams(
             collective_id=0, has_side_effects=True, vmem_limit_bytes=63_000_000

time: 165 us -> 184 us (1.12); the launches traced: 164 us -> 181 us
  Pallas kernels: 159 us -> 175 us
    pallas_call x1, Pallas kernels: 159 us -> 175 us  [on_device(): pl.pallas_call(kernel, out_shape=(jax.ShapeDtypeStruct((LB, Q, Q), BF), j...]
where the time goes in v2:
time: 184 us; the launch traced here: 181 us
  Pallas kernels  175 us (95%)
  local copies, waits for them, and re-layouts  5.06 us (3%)
    pallas_call x1, Pallas kernels, on_device(): pl.pallas_call(kernel, out_shape=(jax.ShapeDtypeStruct((LB, Q, Q), BF), j...  175 us
    unnamed x2, local copies, waits for them, and re-layouts  3.79 us

profile of v2, /device:TPU:1, one launch (start us, length us, event | category | flops | bytes accessed | tf_op | source)
XLA Modules:
  0.0 180.9 jit_solution(5960818024626198401)
XLA Ops:
  0.6 1.3 broadcast_in_dim.6.quad
  1.9 175.2 %shard_map.68 = (bf16[12,128,128]{2,1,0:T(8,128)(2,1)}, bf16[45,64,128]{2,1,0:T(8,128)(2,1)}) custom-call(bf16[45,64,128]{2,1,0:T(8,128)(2,1)} %bitcast.9, bf16[45,64,128]{2,1,0:T(8,128)(2,1)} %bitcast.10, bf16[4,192,720]{2,1,0:T(8,128)(2,1)} %leg.1, f32[1,720]{1,0:T(1,128)} %broadcast_in_dim.6.quad, bf16[12,512,128]{2,1,0:T(8,128)(2,1)} %w.1), custom_call_target="tpu_custom_call" | custom-call | tf_op jit(solution)/shard_map/pallas_call | solution.py:477
  177.1 1.8 copy.9
  178.9 2.0 %copy.10 = bf16[1,64,45,128]{3,1,2,0:T(8,128)(2,1)} copy(bf16[1,64,45,128]{3,1,2,0:T(8,128)(2,1)} %bitcast.11) | data formatting | bytes 1474560

commit v3 on v2

--- a/solution.py
+++ b/solution.py
@@ -35,11 +35,11 @@
 
 def kernel(
     go, si, leg, quad, w, gw, gi,
-    r_syn, r_ana, t_syn, t_ana, p_in, p_sort, p_unsort, w2,
-    g1s, g1r, s1s, s1r, acc, g2s, g2r, s2s, s2r, gall, sall, ks, kr,
-    xa, tsend, trecv, tall, xr, t_back, ag, oacc,
-    g_ss, g_rs, s_ss, s_rs, g2_ss, g2_rs, s2_ss, s2_rs, k_ss, k_rs, d_ss, d_rs, e_ss, e_rs,
-    t_ss, t_rs, a_ss, a_rs, r_ss, r_rs,
+    r_syn, t_syn, p_in, p_sort, p_unsort, p_merge, w2,
+    g1s, g1r, acc, g2s, g2r, gall, sall, ks, kr,
+    xa, tsend, trecv, tall, xr, e_col, e_row, keep_f, keep_b, x8, t_f, own, part_r, t_b, ag, oacc,
+    g_ss, g_rs, g2_ss, g2_rs, k_ss, k_rs, d_ss, d_rs, e_ss, e_rs,
+    t_ss, t_rs, a_ss, a_rs, p_ss, p_rs, r_ss, r_rs,
 ):
     dp, z, ch = lax.axis_index("dp"), lax.axis_index("lat"), lax.axis_index("chan")
     barrier = pltpu.get_barrier_semaphore()
@@ -104,55 +104,55 @@
 
         lax.fori_loop(0, 4, step, 0)
 
-    order_in(go, g1s)
-    pl.semaphore_wait(barrier, NZ - 1 + NDP * NCHAN - 1)
-    z_send(g1s, g1r, g_ss, g_rs, 0, 3)
-
     me = dp * NCHAN + ch
     shares = me < SHARES
     group, pair = jnp.minimum(me // 2, SHARES // 2 - 1), me % 2
     for h in range(2):
-        part = leg[2 * pair + h, pl.ds(pl.multiple_of(16 * group, 16), 16), :].astype(F32)
+        rows = leg[2 * pair + h, pl.ds(pl.multiple_of(16 * group, 16), 16), :].astype(F32)
         xa[h, :, 720:] = jnp.zeros((16, ROWS - 720), BF)
-        xa[h, :, :720] = (part * quad[...]).astype(BF)
+        xa[h, :, :720] = (rows * quad[...].reshape(1, 720)).astype(BF)
 
     def window(zz):
         start = jnp.minimum((zz * J) // 128, 4) * 128
         return pl.ds(pl.multiple_of(start, 128), 256), zz * J - start
 
-    def cut(zz, c):
-        at, off = window(zz)
-        r, k = iota((512, 128), 0), iota((512, 128), 1)
-        pick = one_hot((r % 256 == off + k % 64) & (r // 256 == k // 64) & (k % 64 < J))
-        both = jnp.concatenate([xa[0, :, at], xa[1, :, at]], axis=1)
-        tsend[zz] = dot(both, pick).astype(BF)
-        return c
-
-    lax.fori_loop(0, NZ, cut, 0)
+    def cut(i, c):
+        for u in range(4):
+            zz = 4 * i + u
+            at, off = window(zz)
+            r, k = iota((512, 128), 0), iota((512, 128), 1)
+            pick = one_hot((r % 256 == off + k % 64) & (r // 256 == k // 64) & (k % 64 < J))
+            both = jnp.concatenate([xa[0, :, at], xa[1, :, at]], axis=1)
+            tsend[zz] = dot(both, pick).astype(BF)
+        return c
+
+    lax.fori_loop(0, NZ // 4, cut, 0)
+    order_in(go, g1s)
+    pl.semaphore_wait(barrier, NZ - 1 + NDP * NCHAN - 1)
 
     @pl.when(shares)
     def _():
         z_send(tsend, trecv, t_ss, t_rs, 0, NZ - 1)
 
+    z_send(g1s, g1r, g_ss, g_rs, 0, NZ - 1)
     trecv[z] = tsend[z]
-    z_send(g1s, g1r, g_ss, g_rs, 3, NZ - 1)
-    order_in(si, s1s)
-    z_send(s1s, s1r, s_ss, s_rs, 0, 8, flip=True)
     g1r[z] = g1s[z]
-    s1r[z] = s1s[z]
+
+    x8[:, 8 * J :, :] = jnp.zeros((8, CH * 2 - 8 * J, Q), BF)
+    for k in range(4):
+        rows = si[:, 16 * k : 16 * k + 16, :].astype(F32)
+        for h in range(2):
+            x8[2 * k + h, : 8 * J, :] = rows[:, 8 * h : 8 * h + 8, :].reshape(8 * J, Q).astype(BF)
 
     zero = jnp.zeros((ROWS, ROWS - 720), BF)
     r_syn[:, 720:] = zero
-    r_ana[:, 720:] = zero
 
     def rows_of(ib, c):
         r = iota((128, ROWS), 0) + ib * 128
         pick = one_hot(iota((128, ROWS), 1) == (r % 4) * (NZ * LB) + r // 4)
         flat = leg[...].reshape(ROWS, 720)
         at = pl.ds(pl.multiple_of(ib * 128, 128), 128)
-        syn = dot(pick, flat)
-        r_syn[at, :720] = syn.astype(BF)
-        r_ana[at, :720] = (syn * quad[...]).astype(BF)
+        r_syn[at, :720] = dot(pick, flat).astype(BF)
         return c
 
     lax.fori_loop(0, ROWS // 128, rows_of, 0)
@@ -171,14 +171,39 @@
 
     table(r_syn, t_syn)
 
+    def a_copy(to, frm):
+        return pltpu.make_async_remote_copy(
+            src_ref=trecv, dst_ref=tall.at[frm], send_sem=a_ss.at[to], recv_sem=a_rs.at[frm],
+            device_id={"dp": to // NCHAN, "chan": to % NCHAN}, device_id_type=MESH,
+        )
+
+    @pl.when(shares)
+    def _():
+        z_wait_all(tsend, trecv, t_ss, t_rs)
+
+        def a_send(s, c):
+            a_copy((me + s + 1) % (NDP * NCHAN), me).start()
+            return c
+
+        lax.fori_loop(0, NDP * NCHAN - 1, a_send, 0)
+        tall[me] = trecv[...]
+
     def sort_block(ib, c):
         at = pl.ds(pl.multiple_of(ib * 128, 128), 128)
         r, k = iota((128, ROWS), 0) + ib * 128, iota((128, ROWS), 1)
         p_sort[at, :] = one_hot(k == ((r % M) // 4) * 48 + (r // M) * 4 + r % 4)
+        p_merge[at, :] = one_hot(k == ((r % M) // 8) * 96 + (r // M) * 8 + r % 8)
         p_unsort[at, :] = one_hot(k == ((r % 96) // 8) * M + (r // 96) * 8 + r % 8)
         return c
 
     lax.fori_loop(0, ROWS // 128, sort_block, 0)
+
+    r, k = iota((128, 2 * CH), 0), iota((128, 2 * CH), 1)
+    e_col[...] = one_hot((r == (k % 2) * 64 + k // 8) & (k < 8 * J))
+    r, k = iota((8 * J, 128), 0), iota((8 * J, 128), 1)
+    e_row[...] = one_hot(k == (r % 2) * 64 + r // 8)
+    keep_f[...] = one_hot(iota((CH, 2 * CH), 0) % 8 == iota((CH, 2 * CH), 1) % 8)
+    keep_b[...] = one_hot(iota((8 * J, CH), 0) % 8 == iota((8 * J, CH), 1) % 8)
 
     ra, ca = iota((Q, Q), 0), iota((Q, Q), 1)
     swap = jnp.where(ca == ra + 1, 1.0, 0.0) * jnp.where(ra % 2 == 0, 1.0, 0.0)
@@ -195,30 +220,11 @@
 
     lax.fori_loop(0, LB, weave_weight, 0)
 
-    def a_copy(to, frm):
-        return pltpu.make_async_remote_copy(
-            src_ref=trecv, dst_ref=tall.at[frm], send_sem=a_ss.at[to], recv_sem=a_rs.at[frm],
-            device_id={"dp": to // NCHAN, "chan": to % NCHAN}, device_id_type=MESH,
-        )
-
-    @pl.when(shares)
-    def _():
-        z_wait_all(tsend, trecv, t_ss, t_rs)
-
-        def a_send(s, c):
-            a_copy((me + s + 1) % (NDP * NCHAN), me).start()
-            return c
-
-        lax.fori_loop(0, NDP * NCHAN - 1, a_send, 0)
-        tall[me] = trecv[...]
-
-    table(r_ana, t_ana)
-
-    def legendre_sum(t, send, recv, ss, rs, out, flip=False):
+    def legendre_sum(t, send, recv, ss, rs, out):
         acc[...] = dot(t[z], recv[z])
 
         def step(s, c):
-            frm = z_wait_recv(send, recv, ss, rs, NZ - 2 - s if flip else s)
+            frm = z_wait_recv(send, recv, ss, rs, s)
             acc[...] += dot(t[frm], recv[frm])
             return c
 
@@ -227,8 +233,64 @@
 
     legendre_sum(t_syn, g1s, g1r, g_ss, g_rs, g2s)
     z_send(g2s, g2r, g2_ss, g2_rs, 0, NZ - 1)
-    z_send(s1s, s1r, s_ss, s_rs, 8, NZ - 1, flip=True)
     g2r[z] = g2s[z]
+
+    def a_wait(s, c):
+        @pl.when(s != me)
+        def _():
+            a_copy(s, s).wait_recv()
+
+        return c
+
+    lax.fori_loop(0, SHARES, a_wait, 0)
+    rx, cx = iota((128, 64), 0), iota((128, 64), 1)
+    spread = one_hot(cx == ((rx % 8) // 2) * 16 + rx // 8)
+
+    def by_degree(lg, c):
+        at = pl.ds(pl.multiple_of(lg * 128, 128), 128)
+        for g in range(8):
+            tiles = [tall[2 * lg + t % 2, 2 * g + t // 2] for t in range(4)]
+            xr[g, at, :] = dot(spread, jnp.concatenate(tiles, axis=0)).astype(BF)
+        return c
+
+    lax.fori_loop(0, 12, by_degree, 0)
+
+    def both_of(g, d0, d1):
+        a = xr[g, pl.ds(pl.multiple_of(d0 * 96, 32), 96), :]
+        b = xr[g, pl.ds(pl.multiple_of(d1 * 96, 32), 96), :]
+        return jnp.concatenate([a, b], axis=0)
+
+    def own_terms(d0, d1):
+        for g in range(8):
+            t_f[g] = dot(both_of(g, d0, d1), e_col[...]).astype(BF) * keep_f[...]
+        for g in range(8):
+            own[g] = dot(t_f[g], x8[g])
+
+    def p_copy(side, hop, part):
+        to = (z + (1 if side == 0 else NZ - 1)) % NZ
+        at = pl.ds(2 * part, 2)
+        return pltpu.make_async_remote_copy(
+            src_ref=part_r.at[side, hop - 1, at], dst_ref=part_r.at[side, hop, at],
+            send_sem=p_ss.at[side, hop - 1, part], recv_sem=p_rs.at[side, hop - 1, part],
+            device_id={"lat": to}, device_id_type=MESH,
+        )
+
+    def p_send(side, hop, part, arrived):
+        at = pl.ds(2 * part, 2)
+        value = own[2 * part : 2 * part + 2, 96 * side : 96 * side + 96, :]
+        if arrived:
+            p_copy(side, hop - 1, part).wait_recv()
+            value = value + part_r[side, hop - 1, at].astype(F32)
+        part_r[side, hop - 1, at] = value.astype(BF)
+        p_copy(side, hop, part).start()
+
+    half_way = (z + NZ // 2) % NZ
+    own_terms(half_way, half_way)
+    for part in range(4):
+        p_send(part // 2, 1, part, False)
+    own_terms((z + 7) % NZ, (z + 9) % NZ)
+    for part in range(4):
+        p_send(1 - part // 2, 2, part, False)
     z_wait_all(g2s, g2r, g2_ss, g2_rs)
     grads = dot(p_sort[...], g2r[...].reshape(ROWS, Q)).astype(BF).reshape(LB, M, Q)
     gall[dp] = grads
@@ -266,40 +328,17 @@
     lax.fori_loop(0, NDP - 1, d_send, 0)
     kr[ch] = ks[ch]
 
-    def a_wait(s, c):
-        @pl.when(s != me)
-        def _():
-            a_copy(s, s).wait_recv()
-
-        return c
-
-    lax.fori_loop(0, SHARES, a_wait, 0)
-    rx, cx = iota((128, 64), 0), iota((128, 64), 1)
-    spread = one_hot(cx == ((rx % 8) // 2) * 16 + rx // 8)
-
-    def by_degree(i, c):
-        g, lg = i % 8, i // 8
-        tiles = [tall[2 * lg + t % 2, 2 * g + t // 2] for t in range(4)]
-        at = pl.ds(pl.multiple_of(lg * 128, 128), 128)
-        xr[g, at, :] = dot(spread, jnp.concatenate(tiles, axis=0)).astype(BF)
-        return c
-
-    lax.fori_loop(0, 96, by_degree, 0)
-
-    def back_table(i, c):
-        g, o = i % 8, i // 8
-        r, k = iota((8 * J, 128), 0), iota((8 * J, 128), 1)
-        pick = one_hot(k == (r % 2) * 64 + r // 8)
-        full = dot(pick, xr[g, pl.ds(pl.multiple_of(o * 96, 32), 96), :], ((1,), (1,)))
-        keep = iota((8 * J, 96), 0) % 8 == iota((8 * J, 96), 1) % 8
-        t_back[o, g] = jnp.where(keep, full, 0.0).astype(BF)
-        return c
-
-    lax.fori_loop(0, 8 * NZ, back_table, 0)
-
-    legendre_sum(t_ana, s1s, s1r, s_ss, s_rs, s2s, flip=True)
-    z_send(s2s, s2r, s2_ss, s2_rs, 0, NZ - 1)
-    s2r[z] = s2s[z]
+    for part in range(4):
+        p_send(part // 2, 2, part, True)
+
+    def ring(hop, c):
+        own_terms((z + 9 - hop) % NZ, (z + NZ - 9 + hop) % NZ)
+        for part in range(4):
+            for side in range(2):
+                p_send(side, hop, part, True)
+        return c
+
+    lax.fori_loop(3, NZ // 2 + 1, ring, 0)
 
     def k_wait(s, c):
         frm = (ch + s + 1) % NCHAN
@@ -332,9 +371,17 @@
             r_copy(side, 0, part, z).start()
 
     home, half = ch // 2, ch % 2
-    z_wait_all(s2s, s2r, s2_ss, s2_rs)
     mine = sall.at[dp, half]
-    spectra = dot(p_sort[...], s2r[...].reshape(ROWS, Q)).astype(BF).reshape(LB, M, Q)
+    own_terms(z, z)
+    for part in range(4):
+        at = pl.ds(2 * part, 2)
+        value = own[2 * part : 2 * part + 2, :96, :]
+        for side in range(2):
+            p_copy(side, NZ // 2, part).wait_recv()
+            value = value + part_r[side, NZ // 2, at].astype(F32)
+        part_r[0, NZ // 2, at] = value.astype(BF)
+    merged = part_r[0, NZ // 2].reshape(ROWS, Q)
+    spectra = dot(p_merge[...], merged).astype(BF).reshape(LB, M, Q)
     s2all = ks.at[ch]
     s2all[...] = spectra
 
@@ -359,11 +406,17 @@
     def _():
         mine[...] = spectra
 
+    def back_terms(d0, d1):
+        for g in range(8):
+            t_b[g] = dot(e_row[...], both_of(g, d0, d1), ((1,), (1,))).astype(BF) * keep_b[...]
+
+    back_terms(z, half_way)
     for g in range(8):
-        oacc[g] = dot(t_back[z, g], ag[z, g])
+        oacc[g] = dot(t_b[g, :, :96], ag[z, g])
 
     def hop_in(k, c):
         left, right = (z + NZ - k) % NZ, (z + k) % NZ
+        back_terms(left, right)
         for part in range(4):
             for side, origin in ((0, left), (1, right)):
                 r_copy(side, k - 1, part, origin).wait_recv()
@@ -376,7 +429,7 @@
                         r_copy(side, k, part, origin).start()
 
             for g in (2 * part, 2 * part + 1):
-                oacc[g] += dot(t_back[left, g], ag[left, g]) + dot(t_back[right, g], ag[right, g])
+                oacc[g] += dot(t_b[g], jnp.concatenate([ag[left, g], ag[right, g]], axis=0))
         return c
 
     lax.fori_loop(1, NZ // 2, hop_in, 0)
@@ -411,19 +464,26 @@
 
     lax.fori_loop(0, LB, weight, 0)
 
-    across = (z + NZ // 2) % NZ
-    for part in range(4):
-        r_copy(part // 2, NZ // 2 - 1, part, across).wait_recv()
+    back_terms(half_way, half_way)
+    for part in range(4):
+        r_copy(part // 2, NZ // 2 - 1, part, half_way).wait_recv()
         halves = []
         for g in (2 * part, 2 * part + 1):
-            halves.append((oacc[g] + dot(t_back[across, g], ag[across, g])).reshape(J, 8, Q))
+            halves.append((oacc[g] + dot(t_b[g, :, :96], ag[half_way, g])).reshape(J, 8, Q))
         gi[:, pl.ds(16 * part, 16), :] = jnp.concatenate(halves, axis=1).astype(BF)
 
-    for args in (
-        (g1s, g1r, g_ss, g_rs), (s1s, s1r, s_ss, s_rs), (g2s, g2r, g2_ss, g2_rs),
-        (s2s, s2r, s2_ss, s2_rs),
-    ):
-        z_wait_sends(*args)
+    z_wait_sends(g1s, g1r, g_ss, g_rs)
+    z_wait_sends(g2s, g2r, g2_ss, g2_rs)
+
+    def p_done(hop, c):
+        for part in range(4):
+            for side in range(2):
+                p_copy(side, hop, part).wait_send()
+        return c
+
+    lax.fori_loop(2, NZ // 2 + 1, p_done, 0)
+    for part in range(4):
+        p_copy(part // 2, 1, part).wait_send()
 
     @pl.when(shares)
     def _():
@@ -483,31 +543,31 @@
         in_specs=[vmem] * 5,
         out_specs=(vmem, vmem),
         scratch_shapes=[
-            pltpu.VMEM((ROWS, ROWS), BF), pltpu.VMEM((ROWS, ROWS), BF),
-            pltpu.VMEM((NZ, ROWS, CH), BF), pltpu.VMEM((NZ, ROWS, CH), BF),
+            pltpu.VMEM((ROWS, ROWS), BF), pltpu.VMEM((NZ, ROWS, CH), BF),
             pltpu.VMEM((4 * CH, 16 * J), BF),
-            pltpu.VMEM((ROWS, ROWS), BF), pltpu.VMEM((ROWS, ROWS), BF),
+            pltpu.VMEM((ROWS, ROWS), BF), pltpu.VMEM((ROWS, ROWS), BF), pltpu.VMEM((ROWS, ROWS), BF),
             pltpu.VMEM((LB, 1024, Q), BF),
             pltpu.VMEM((NZ, CH, Q), BF), pltpu.VMEM((NZ, CH, Q), BF),
-            pltpu.VMEM((NZ, CH, Q), BF), pltpu.VMEM((NZ, CH, Q), BF),
             pltpu.VMEM((ROWS, Q), F32),
-            pltpu.VMEM((NZ, LB * MB, Q), BF), pltpu.VMEM((NZ, LB * MB, Q), BF),
             pltpu.VMEM((NZ, LB * MB, Q), BF), pltpu.VMEM((NZ, LB * MB, Q), BF),
             pltpu.VMEM((NDP, LB, M, Q), BF), pltpu.VMEM((NDP, 2, LB, M, Q), BF),
             pltpu.VMEM((NCHAN, LB, M, Q), BF), pltpu.VMEM((NCHAN, LB, M, Q), BF),
             pltpu.VMEM((2, 16, ROWS), BF), pltpu.VMEM((NZ, 16, 128), BF), pltpu.VMEM((NZ, 16, 128), BF),
             pltpu.VMEM((SHARES, NZ, 16, 128), BF), pltpu.VMEM((8, 8 * CH, 128), BF),
-            pltpu.VMEM((NZ, 8, 8 * J, 96), BF), pltpu.VMEM((NZ, 8, 96, Q), BF),
-            pltpu.VMEM((8, 8 * J, Q), F32),
-            dma((NZ,)), dma((NZ,)), dma((NZ,)), dma((NZ,)), dma((NZ,)), dma((NZ,)),
-            dma((NZ,)), dma((NZ,)), dma((NCHAN,)), dma((NCHAN,)), dma((NDP,)), dma((NDP,)),
-            dma((NCHAN,)), dma((NDP, 2)), dma((NZ,)), dma((NZ,)),
-            dma((NDP * NCHAN,)), dma((SHARES,)), dma((2, NZ // 2, 4)), dma((2, NZ // 2, 4)),
+            pltpu.VMEM((128, 2 * CH), BF), pltpu.VMEM((8 * J, 128), BF),
+            pltpu.VMEM((CH, 2 * CH), BF), pltpu.VMEM((8 * J, CH), BF),
+            pltpu.VMEM((8, 2 * CH, Q), BF), pltpu.VMEM((8, CH, 2 * CH), BF), pltpu.VMEM((8, CH, Q), F32),
+            pltpu.VMEM((2, NZ // 2 + 1, 8, 96, Q), BF), pltpu.VMEM((8, 8 * J, CH), BF),
+            pltpu.VMEM((NZ, 8, 96, Q), BF), pltpu.VMEM((8, 8 * J, Q), F32),
+            dma((NZ,)), dma((NZ,)), dma((NZ,)), dma((NZ,)),
+            dma((NCHAN,)), dma((NCHAN,)), dma((NDP,)), dma((NDP,)), dma((NCHAN,)), dma((NDP, 2)),
+            dma((NZ,)), dma((NZ,)), dma((NDP * NCHAN,)), dma((SHARES,)),
+            dma((2, NZ // 2, 4)), dma((2, NZ // 2, 4)), dma((2, NZ // 2, 4)), dma((2, NZ // 2, 4)),
         ],
         compiler_params=pltpu.CompilerParams(
             collective_id=0, has_side_effects=True, vmem_limit_bytes=63_000_000
         ),
-    )(go, si, legendre, quad_weight[None, :], mixing_weight)
+    )(go, si, legendre, quad_weight, mixing_weight)
     return gw, gi.transpose(1, 0, 2)[None]
 
 

time: 184 us -> 152 us (0.83)
  the two profiles are of different devices: /device:TPU:1 before, /device:TPU:8 now
where the time goes in v3:
time: 152 us; the launch traced here: 151 us
  Pallas kernels  147 us (97%)
  local copies, waits for them, and re-layouts  3.79 us (2%)
    pallas_call x1, Pallas kernels, on_device(): pl.pallas_call(kernel, out_shape=(jax.ShapeDtypeStruct((LB, Q, Q), BF), j...  147 us
    unnamed x2, local copies, waits for them, and re-layouts  3.79 us

profile of v3, /device:TPU:8, one launch (start us, length us, event | category | flops | bytes accessed | tf_op | source)
XLA Modules:
  0.0 151.5 jit_solution(9919009626527478151)
XLA Ops:
  0.6 147.1 %shard_map.68 = (bf16[12,128,128]{2,1,0:T(8,128)(2,1)}, bf16[45,64,128]{2,1,0:T(8,128)(2,1)}) custom-call(bf16[45,64,128]{2,1,0:T(8,128)(2,1)} %bitcast.9, bf16[45,64,128]{2,1,0:T(8,128)(2,1)} %bitcast.10, bf16[4,192,720]{2,1,0:T(8,128)(2,1)} %leg.1, f32[720]{0:T(1024)} %quad.1, bf16[12,512,128]{2,1,0:T(8,128)(2,1)} %w.1), custom_call_target="tpu_custom_call" | custom-call | tf_op jit(solution)/shard_map/pallas_call | solution.py:537
  147.7 1.8 %copy.9 = bf16[12,128,128]{2,1,0:T(8,128)(2,1)} copy(bf16[12,128,128]{2,1,0:T(8,128)(2,1)} %get-tuple-element.8) | data formatting | bytes 786432
  149.5 2.0 %copy.10 = bf16[1,64,45,128]{3,1,2,0:T(8,128)(2,1)} copy(bf16[1,64,45,128]{3,1,2,0:T(8,128)(2,1)} %bitcast.11) | data formatting | bytes 1474560

commit v4 on v3

v4 whole, which is shorter than its diff:
```python
import jax
import jax.numpy as jnp
from jax import lax
from jax.experimental import pallas as pl
from jax.experimental.pallas import tpu as pltpu
from jax.sharding import PartitionSpec as P

MESH = pl.DeviceIdType.MESH
BF = jnp.bfloat16
F32 = jnp.float32

M, J, Q, LB, MB, CH, NZ = 64, 45, 128, 12, 4, 192, 16
ROWS = NZ * LB * MB
NCHAN, NDP = 8, 4
SHARES = 24


def iota(shape, dim):
    return lax.broadcasted_iota(jnp.int32, shape, dim)


def dot(a, b, dims=((1,), (0,))):
    return lax.dot_general(a, b, (dims, ((), ())), preferred_element_type=F32)


def static_one(hop):
    return isinstance(hop, int) and hop == 1


def one_hot(hit):
    return jnp.where(hit, 1.0, 0.0).astype(BF)


def offset_of(s):
    k = (s + 1) // 2
    far = 8 - k
    return jnp.where(s % 2 == 1, far, NZ - far)


def kernel(
    go_in, si_in, leg_in, quad, w_in, gw, gi,
    go, si, leg, w, in_sem,
    r_syn, t_syn, p_in, p_sort, p_unsort, p_merge, w2,
    g1s, g1r, acc, g2s, g2r, gall, sall, ks, kr,
    xa, tsend, trecv, tall, xr, e_col, e_row, keep_f, keep_b, x8, t_f, own, part_r, t_b, ag, oacc, gpart,
    g_ss, g_rs, g2_ss, g2_rs, k_ss, k_rs, d_ss, d_rs, e_ss, e_rs, e1_rs, f_ss,
    t_ss, t_rs, a_ss, a_rs, p_ss, p_rs, r_ss, r_rs,
):
    dp, z, ch = lax.axis_index("dp"), lax.axis_index("lat"), lax.axis_index("chan")
    barrier = pltpu.get_barrier_semaphore()
    loads = [
        pltpu.make_async_copy(src, dst, in_sem.at[n])
        for n, (src, dst) in enumerate(((leg_in, leg), (go_in, go), (si_in, si), (w_in, w)))
    ]
    for load in loads:
        load.start()

    def greet_z(s, c):
        to = (z + s + 1) % NZ
        pl.semaphore_signal(barrier, inc=1, device_id={"lat": to}, device_id_type=MESH)
        return c

    def greet_plane(s, c):
        other = (dp * NCHAN + ch + s + 1) % (NDP * NCHAN)
        pl.semaphore_signal(
            barrier, inc=1, device_id={"dp": other // NCHAN, "chan": other % NCHAN}, device_id_type=MESH
        )
        return c

    lax.fori_loop(0, NZ - 1, greet_z, 0)
    lax.fori_loop(0, NDP * NCHAN - 1, greet_plane, 0)

    def z_copy(src, dst, ss, rs, to, slot):
        return pltpu.make_async_remote_copy(
            src_ref=src.at[to], dst_ref=dst.at[slot], send_sem=ss.at[0],
            recv_sem=rs.at[slot if rs.shape[0] > 1 else 0],
            device_id={"lat": to}, device_id_type=MESH,
        )

    def z_send(src, dst, ss, rs, first, last):
        def step(s, c):
            z_copy(src, dst, ss, rs, (z + offset_of(s)) % NZ, z).start()
            return c

        lax.fori_loop(first, last, step, 0)

    def batch(ref, count, ss, rs):
        at = ref if count is None else ref.at[pl.ds(0, count)]
        return pltpu.make_async_remote_copy(
            src_ref=at, dst_ref=at, send_sem=ss, recv_sem=rs,
            device_id={"lat": (z + 1) % NZ}, device_id_type=MESH,
        )

    for zz in range(4):
        r, c = iota((CH, 16 * J), 0), iota((CH, 16 * J), 1)
        p_in[pl.ds(zz * CH, CH), :] = one_hot((c == (r // 4) * 16 + zz * 4 + r % 4) & (r < MB * J))

    def order_in(x, out):
        def step(g, c):
            rows = x[:, pl.ds(pl.multiple_of(16 * g, 16), 16), :].reshape(16 * J, Q)
            out[pl.ds(4 * g, 4)] = dot(p_in[...], rows).astype(BF).reshape(4, CH, Q)
            return c

        lax.fori_loop(0, 4, step, 0)

    me = dp * NCHAN + ch
    shares = me < SHARES
    group, pair = jnp.minimum(me // 2, SHARES // 2 - 1), me % 2
    loads[0].wait()
    for h in range(2):
        rows = leg[2 * pair + h, pl.ds(pl.multiple_of(16 * group, 16), 16), :].astype(F32)
        xa[h, :, 720:] = jnp.zeros((16, ROWS - 720), BF)
        xa[h, :, :720] = (rows * quad[...].reshape(1, 720)).astype(BF)

    def window(zz):
        start = jnp.minimum((zz * J) // 128, 4) * 128
        return pl.ds(pl.multiple_of(start, 128), 256), zz * J - start

    def cut(i, c):
        for u in range(4):
            zz = 4 * i + u
            at, off = window(zz)
            r, k = iota((512, 128), 0), iota((512, 128), 1)
            pick = one_hot((r % 256 == off + k % 64) & (r // 256 == k // 64) & (k % 64 < J))
            both = jnp.concatenate([xa[0, :, at], xa[1, :, at]], axis=1)
            tsend[zz] = dot(both, pick).astype(BF)
        return c

    loads[1].wait()
    order_in(go, g1s)
    pl.semaphore_wait(barrier, NZ - 1 + NDP * NCHAN - 1)
    z_send(g1s, g1r, g_ss, g_rs, 0, 1)
    lax.fori_loop(0, NZ // 4, cut, 0)

    @pl.when(shares)
    def _():
        z_send(tsend, trecv, t_ss, t_rs, 0, NZ - 1)

    z_send(g1s, g1r, g_ss, g_rs, 1, NZ - 1)
    trecv[z] = tsend[z]
    g1r[z] = g1s[z]

    loads[2].wait()
    x8[:, 8 * J :, :] = jnp.zeros((8, CH * 2 - 8 * J, Q), BF)
    for k in range(4):
        rows = si[:, 16 * k : 16 * k + 16, :].astype(F32)
        for h in range(2):
            x8[2 * k + h, : 8 * J, :] = rows[:, 8 * h : 8 * h + 8, :].reshape(8 * J, Q).astype(BF)

    zero = jnp.zeros((ROWS, ROWS - 720), BF)
    r_syn[:, 720:] = zero

    def rows_of(ib, c):
        r = iota((128, ROWS), 0) + ib * 128
        pick = one_hot(iota((128, ROWS), 1) == (r % 4) * (NZ * LB) + r // 4)
        flat = leg[...].reshape(ROWS, 720)
        at = pl.ds(pl.multiple_of(ib * 128, 128), 128)
        r_syn[at, :720] = dot(pick, flat).astype(BF)
        return c

    lax.fori_loop(0, ROWS // 128, rows_of, 0)

    def table(src, dst):
        def step(zz, c):
            at, off = window(zz)
            r, k = iota((256, CH), 0), iota((256, CH), 1)
            pick = one_hot((r == off + k // 4) & (k < MB * J))
            full = dot(src[:, at], pick)
            keep = iota((ROWS, CH), 0) % 4 == iota((ROWS, CH), 1) % 4
            dst[zz] = jnp.where(keep, full, 0.0).astype(BF)
            return c

        lax.fori_loop(0, NZ, step, 0)

    table(r_syn, t_syn)

    def a_copy(to, s):
        return pltpu.make_async_remote_copy(
            src_ref=trecv, dst_ref=tall.at[me], send_sem=a_ss.at[s // SHARES], recv_sem=a_rs.at[0],
            device_id={"dp": to // NCHAN, "chan": to % NCHAN}, device_id_type=MESH,
        )

    @pl.when(shares)
    def _():
        batch(trecv, NZ - 1, t_ss.at[0], t_rs.at[0]).wait_recv()

        def a_send(s, c):
            a_copy((me + s + 1) % (NDP * NCHAN), s).start()
            return c

        lax.fori_loop(0, NDP * NCHAN - 1, a_send, 0)
        tall[me] = trecv[...]

    def sort_block(ib, c):
        at = pl.ds(pl.multiple_of(ib * 128, 128), 128)
        r, k = iota((128, ROWS), 0) + ib * 128, iota((128, ROWS), 1)
        p_sort[at, :] = one_hot(k == ((r % M) // 4) * 48 + (r // M) * 4 + r % 4)
        p_merge[at, :] = one_hot(k == ((r % M) // 8) * 96 + (r // M) * 8 + r % 8)
        p_unsort[at, :] = one_hot(k == ((r % 96) // 8) * M + (r // 96) * 8 + r % 8)
        return c

    lax.fori_loop(0, ROWS // 128, sort_block, 0)

    r, k = iota((128, 2 * CH), 0), iota((128, 2 * CH), 1)
    e_col[...] = one_hot((r == (k % 2) * 64 + k // 8) & (k < 8 * J))
    r, k = iota((8 * J, 128), 0), iota((8 * J, 128), 1)
    e_row[...] = one_hot(k == (r % 2) * 64 + r // 8)
    keep_f[...] = one_hot(iota((CH, 2 * CH), 0) % 8 == iota((CH, 2 * CH), 1) % 8)
    keep_b[...] = one_hot(iota((8 * J, CH), 0) % 8 == iota((8 * J, CH), 1) % 8)

    ra, ca = iota((Q, Q), 0), iota((Q, Q), 1)
    swap = jnp.where(ca == ra + 1, 1.0, 0.0) * jnp.where(ra % 2 == 0, 1.0, 0.0)
    swap = (swap - jnp.where(ra == ca + 1, 1.0, 0.0) * jnp.where(ca % 2 == 0, 1.0, 0.0)).astype(BF)
    r2, c2 = iota((256, 256), 0), iota((256, 256), 1)
    weave = one_hot(c2 == (r2 % 2) * 128 + r2 // 2)

    def weave_weight(l, c):
        for k in range(4):
            block = w[l, pl.ds(128 * k, 128), :]
            both = jnp.concatenate([block, dot(block, swap).astype(BF)], axis=0)
            w2[l, pl.ds(256 * k, 256), :] = dot(weave, both).astype(BF)
        return c

    loads[3].wait()
    lax.fori_loop(0, LB, weave_weight, 0)

    acc[...] = dot(t_syn[z], g1r[z])

    def latitudes(s, c):
        frm = (z + NZ - offset_of(s)) % NZ
        z_copy(g1s, g1r, g_ss, g_rs, frm, frm).wait_recv()
        acc[...] += dot(t_syn[frm], g1r[frm])
        return c

    lax.fori_loop(0, 11, latitudes, 0)

    @pl.when(shares)
    def _():
        batch(tall, SHARES - 1, a_ss.at[0], a_rs.at[0]).wait_recv()

    @pl.when(jnp.logical_not(shares))
    def _():
        batch(tall, None, a_ss.at[0], a_rs.at[0]).wait_recv()

    rx, cx = iota((128, 64), 0), iota((128, 64), 1)
    spread = one_hot(cx == ((rx % 8) // 2) * 16 + rx // 8)

    def by_degree(lg, c):
        at = pl.ds(pl.multiple_of(lg * 128, 128), 128)
        for g in range(8):
            tiles = [tall[2 * lg + t % 2, 2 * g + t // 2] for t in range(4)]
            xr[g, at, :] = dot(spread, jnp.concatenate(tiles, axis=0)).astype(BF)
        return c

    lax.fori_loop(0, 12, by_degree, 0)

    def both_of(g, d0, d1):
        a = xr[g, pl.ds(pl.multiple_of(d0 * 96, 32), 96), :]
        b = xr[g, pl.ds(pl.multiple_of(d1 * 96, 32), 96), :]
        return jnp.concatenate([a, b], axis=0)

    def own_terms(d0, d1):
        for g in range(8):
            t_f[g] = dot(both_of(g, d0, d1), e_col[...]).astype(BF) * keep_f[...]
        for g in range(8):
            own[g] = dot(t_f[g], x8[g])

    def p_copy(side, hop, part):
        to = (z + (1 if side == 0 else NZ - 1)) % NZ
        at = pl.ds(2 * part, 2)
        return pltpu.make_async_remote_copy(
            src_ref=part_r.at[side, hop - 1, at], dst_ref=part_r.at[side, hop, at],
            send_sem=p_ss.at[side, 0 if static_one(hop) else 1], recv_sem=p_rs.at[side, hop - 1, part],
            device_id={"lat": to}, device_id_type=MESH,
        )

    def p_send(side, hop, part, arrived):
        at = pl.ds(2 * part, 2)
        value = own[2 * part : 2 * part + 2, 96 * side : 96 * side + 96, :]
        if arrived:
            p_copy(side, hop - 1, part).wait_recv()
            value = value + part_r[side, hop - 1, at].astype(F32)
        part_r[side, hop - 1, at] = value.astype(BF)
        p_copy(side, hop, part).start()

    half_way = (z + NZ // 2) % NZ
    own_terms(half_way, half_way)
    for part in range(4):
        p_send(part // 2, 1, part, False)
    own_terms((z + 7) % NZ, (z + 9) % NZ)
    for part in range(4):
        p_send(1 - part // 2, 2, part, False)

    lax.fori_loop(11, NZ - 1, latitudes, 0)
    g2s[...] = acc[...].astype(BF).reshape(NZ, LB * MB, Q)
    z_send(g2s, g2r, g2_ss, g2_rs, 0, NZ - 1)
    g2r[z] = g2s[z]

    for part in range(4):
        p_send(part // 2, 2, part, True)
    own_terms((z + 6) % NZ, (z + 10) % NZ)
    batch(g2r, NZ - 1, g2_ss.at[0], g2_rs.at[0]).wait_recv()
    grads = dot(p_sort[...], g2r[...].reshape(ROWS, Q)).astype(BF).reshape(LB, M, Q)
    gall[dp] = grads

    def mix(n, c):
        for l in (3 * n, 3 * n + 1, 3 * n + 2):
            full = dot(gall[dp, l], w2[l], ((1,), (1,))).astype(BF)
            for k in range(NCHAN):
                ks[k, l] = full[:, 128 * k : 128 * k + 128]
        return c

    lax.fori_loop(0, LB // 3, mix, 0)

    def k_copy(to, slot):
        return pltpu.make_async_remote_copy(
            src_ref=ks.at[to], dst_ref=kr.at[slot], send_sem=k_ss.at[0], recv_sem=k_rs.at[0],
            device_id={"chan": to}, device_id_type=MESH,
        )

    def k_send(s, c):
        k_copy((ch + s + 1) % NCHAN, ch).start()
        return c

    lax.fori_loop(0, NCHAN - 1, k_send, 0)

    kr[ch] = ks[ch]

    def ring(hop, c):
        for part in range(4):
            for side in range(2):
                p_send(side, hop, part, True)
        own_terms((z + 8 - hop) % NZ, (z + NZ - 8 + hop) % NZ)

        @pl.when(hop == 5)
        def _():
            batch(g1s, NZ - 1, g_ss.at[0], g_rs.at[0]).wait_send()
            batch(g2s, NZ - 1, g2_ss.at[0], g2_rs.at[0]).wait_send()

        @pl.when((hop == 6) & shares)
        def _():
            batch(tsend, NZ - 1, t_ss.at[0], t_rs.at[0]).wait_send()
            batch(tall, None, a_ss.at[0], a_rs.at[0]).wait_send()
            batch(tall, NDP * NCHAN - 1 - SHARES, a_ss.at[1], a_rs.at[0]).wait_send()

        return c

    lax.fori_loop(3, NZ // 2 + 1, ring, 0)

    batch(kr, NCHAN - 1, k_ss.at[0], k_rs.at[0]).wait_recv()

    def sum_terms(l, c):
        total = kr[0, l].astype(F32)
        for k in range(1, NCHAN):
            total = total + kr[k, l].astype(F32)
        kr[0, l] = total.astype(BF)
        return c

    lax.fori_loop(0, LB, sum_terms, 0)
    ag[z] = dot(p_unsort[...], kr[0].reshape(ROWS, Q)).astype(BF).reshape(8, 96, Q)

    def r_copy(side, hop, part, origin, last=False):
        to = (z + (1 if side == 0 else NZ - 1)) % NZ
        at = pl.ds(2 * part, 2)
        return pltpu.make_async_remote_copy(
            src_ref=ag.at[origin, at], dst_ref=ag.at[origin, at],
            send_sem=r_ss.at[side, 1 if last else 0], recv_sem=r_rs.at[side, hop, part],
            device_id={"lat": to}, device_id_type=MESH,
        )

    for part in range(4):
        for side in range(2):
            r_copy(side, 0, part, z).start()

    def d_copy(to, slot):
        return pltpu.make_async_remote_copy(
            src_ref=gall.at[dp], dst_ref=gall.at[slot], send_sem=d_ss.at[0], recv_sem=d_rs.at[0],
            device_id={"dp": to}, device_id_type=MESH,
        )

    def d_send(s, c):
        d_copy((dp + s + 1) % NDP, dp).start()
        return c

    lax.fori_loop(0, NDP - 1, d_send, 0)
    home, half, row, col = ch // 2, ch % 2, ch // 4, ch % 4
    relay = (col // 2) == (dp % 2)
    own_relay = home == dp
    mine = sall.at[dp, half]
    for part in range(4):
        at = pl.ds(2 * part, 2)
        value = own[2 * part : 2 * part + 2, :96, :]
        for side in range(2):
            p_copy(side, NZ // 2, part).wait_recv()
            value = value + part_r[side, NZ // 2, at].astype(F32)
        part_r[0, NZ // 2, at] = value.astype(BF)
    merged = part_r[0, NZ // 2].reshape(ROWS, Q)
    spectra = dot(p_merge[...], merged).astype(BF)
    spectra = dot(spectra, one_hot(ra == 2 * (ca % 64) + ca // 64)).astype(BF).reshape(LB, M, Q)
    s2all = ks.at[ch]
    s2all[...] = spectra

    def e_copy(src, dst, h, to, ss, rs):
        return pltpu.make_async_remote_copy(
            src_ref=src, dst_ref=dst, send_sem=ss, recv_sem=rs,
            device_id={"dp": h, "chan": to}, device_id_type=MESH,
        )

    for h in range(2):

        @pl.when(jnp.logical_not(own_relay & (row == h)))
        def _():
            e_copy(ks.at[ch], sall.at[dp, half], home, 4 * h + col, e_ss.at[0], e1_rs.at[dp]).start()

    for h in range(2):
        to = 4 * h + (col + 2) % 4
        e_copy(ks.at[ch], sall.at[dp, half], home, to, e_ss.at[0], e_rs.at[0]).start()

    @pl.when(own_relay)
    def _():
        mine[...] = spectra

    def pass_on():
        for b in range(NDP):
            block = sall.at[b, half]

            @pl.when(jnp.logical_not(own_relay & (dp == b)))
            def _():
                e_copy(block, block, dp, ch, f_ss.at[0], e1_rs.at[b]).wait_recv()

            for side in (1, 3):
                e_copy(block, block, dp, 4 * row + (col + side) % 4, f_ss.at[0], e_rs.at[0]).start()

    def back_terms(d0, d1):
        for g in range(8):
            t_b[g] = dot(e_row[...], both_of(g, d0, d1), ((1,), (1,))).astype(BF) * keep_b[...]

    back_terms(z, half_way)
    for g in range(8):
        oacc[g] = dot(t_b[g, :, :96], ag[z, g])
    back_terms((z + NZ - 1) % NZ, (z + 1) % NZ)

    partner_of = (-swap.astype(F32)).astype(BF)

    def hop_in(k, c):
        left, right = (z + NZ - k) % NZ, (z + k) % NZ
        for part in range(4):
            for side, origin in ((0, left), (1, right)):
                r_copy(side, k - 1, part, origin).wait_recv()
                if part // 2 == side:

                    @pl.when(k < NZ // 2 - 1)
                    def _():
                        r_copy(side, k, part, origin).start()

                    @pl.when(k == NZ // 2 - 1)
                    def _():
                        r_copy(side, k, part, origin, True).start()

                else:

                    @pl.when(k < NZ // 2 - 1)
                    def _():
                        r_copy(side, k, part, origin).start()

            for g in (2 * part, 2 * part + 1):
                oacc[g] += dot(t_b[g], jnp.concatenate([ag[left, g], ag[right, g]], axis=0))
        back_terms((z + NZ - 1 - k) % NZ, (z + 1 + k) % NZ)

        @pl.when(k == 2)
        def _():
            batch(kr, NCHAN - 1, k_ss.at[0], k_rs.at[0]).wait_send()
            for side in range(2):
                batch(part_r.at[side], 7, p_ss.at[side, 1], p_rs.at[side, 0, 0]).wait_send()
                batch(part_r.at[side, 0], 4, p_ss.at[side, 0], p_rs.at[side, 0, 0]).wait_send()

        @pl.when((k == 4) & relay)
        def _():
            pass_on()

        @pl.when(k == 5)
        def _():
            batch(gall, NDP - 1, d_ss.at[0], d_rs.at[0]).wait_recv()
            for b in range(NDP):
                gpart[b] = dot(gall[b].reshape(ROWS, Q), partner_of).astype(BF).reshape(LB, M, Q)

        return c

    lax.fori_loop(1, NZ // 2, hop_in, 0)

    @pl.when(relay)
    def _():
        batch(sall, 2, e_ss.at[0], e_rs.at[0]).wait_recv()

    @pl.when(jnp.logical_not(relay))
    def _():
        batch(sall, None, e_ss.at[0], e_rs.at[0]).wait_recv()

    def weight(n, c):
        for l in (3 * n, 3 * n + 1, 3 * n + 2):
            right = jnp.concatenate(
                [jnp.concatenate([gall[b, l], gpart[b, l]], axis=1) for b in range(NDP)], axis=0
            )
            for h in range(2):
                left = jnp.concatenate([sall[b, h, l] for b in range(NDP)], axis=0)
                total = dot(left, right, ((0,), (0,)))
                gw[l, 64 * h : 64 * h + 64, :] = (
                    (total[:64, :Q] + total[64:, Q:]) * 0.25
                ).astype(BF)
        return c

    lax.fori_loop(0, LB // 3, weight, 0)

    for part in range(4):
        r_copy(part // 2, NZ // 2 - 1, part, half_way).wait_recv()
        halves = []
        for g in (2 * part, 2 * part + 1):
            halves.append((oacc[g] + dot(t_b[g, :, :96], ag[half_way, g])).reshape(J, 8, Q))
        gi[:, pl.ds(16 * part, 16), :] = jnp.concatenate(halves, axis=1).astype(BF)

    for side in range(2):
        batch(ag, 7, r_ss.at[side, 0], r_rs.at[side, 0, 0]).wait_send()
        batch(ag.at[0], 4, r_ss.at[side, 1], r_rs.at[side, 0, 0]).wait_send()
    batch(gall, NDP - 1, d_ss.at[0], d_rs.at[0]).wait_send()

    @pl.when(own_relay)
    def _():
        batch(ks, 3, e_ss.at[0], e_rs.at[0]).wait_send()

    @pl.when(jnp.logical_not(own_relay))
    def _():
        batch(ks, 4, e_ss.at[0], e_rs.at[0]).wait_send()

    @pl.when(relay)
    def _():
        batch(ks, None, f_ss.at[0], e_rs.at[0]).wait_send()


def on_device(saved_input, grad_output, legendre, quad_weight, mixing_weight):
    hbm = pl.BlockSpec(memory_space=pltpu.HBM)
    go = grad_output[0].transpose(1, 0, 2)
    si = saved_input[0].transpose(1, 0, 2)
    vmem = pl.BlockSpec(memory_space=pltpu.VMEM)
    dma = pltpu.SemaphoreType.DMA
    gw, gi = pl.pallas_call(
        kernel,
        out_shape=(
            jax.ShapeDtypeStruct((LB, Q, Q), BF),
            jax.ShapeDtypeStruct((J, M, Q), BF),
        ),
        in_specs=[hbm, hbm, hbm, vmem, hbm],
        out_specs=(vmem, vmem),
        scratch_shapes=[
            pltpu.VMEM((J, M, Q), BF), pltpu.VMEM((J, M, Q), BF),
            pltpu.VMEM((MB, CH, 720), BF), pltpu.VMEM((LB, 512, Q), BF), dma((4,)),
            pltpu.VMEM((ROWS, ROWS), BF), pltpu.VMEM((NZ, ROWS, CH), BF),
            pltpu.VMEM((4 * CH, 16 * J), BF),
            pltpu.VMEM((ROWS, ROWS), BF), pltpu.VMEM((ROWS, ROWS), BF), pltpu.VMEM((ROWS, ROWS), BF),
            pltpu.VMEM((LB, 1024, Q), BF),
            pltpu.VMEM((NZ, CH, Q), BF), pltpu.VMEM((NZ, CH, Q), BF),
            pltpu.VMEM((ROWS, Q), F32),
            pltpu.VMEM((NZ, LB * MB, Q), BF), pltpu.VMEM((NZ, LB * MB, Q), BF),
            pltpu.VMEM((NDP, LB, M, Q), BF), pltpu.VMEM((NDP, 2, LB, M, Q), BF),
            pltpu.VMEM((NCHAN, LB, M, Q), BF), pltpu.VMEM((NCHAN, LB, M, Q), BF),
            pltpu.VMEM((2, 16, ROWS), BF), pltpu.VMEM((NZ, 16, 128), BF), pltpu.VMEM((NZ, 16, 128), BF),
            pltpu.VMEM((SHARES, NZ, 16, 128), BF), pltpu.VMEM((8, 8 * CH, 128), BF),
            pltpu.VMEM((128, 2 * CH), BF), pltpu.VMEM((8 * J, 128), BF),
            pltpu.VMEM((CH, 2 * CH), BF), pltpu.VMEM((8 * J, CH), BF),
            pltpu.VMEM((8, 2 * CH, Q), BF), pltpu.VMEM((8, CH, 2 * CH), BF), pltpu.VMEM((8, CH, Q), F32),
            pltpu.VMEM((2, NZ // 2 + 1, 8, 96, Q), BF), pltpu.VMEM((8, 8 * J, CH), BF),
            pltpu.VMEM((NZ, 8, 96, Q), BF), pltpu.VMEM((8, 8 * J, Q), F32),
            pltpu.VMEM((NDP, LB, M, Q), BF),
            dma((1,)), dma((NZ,)), dma((1,)), dma((1,)), dma((1,)), dma((1,)), dma((1,)), dma((1,)),
            dma((1,)), dma((1,)), dma((NDP,)), dma((1,)), dma((1,)), dma((1,)), dma((2,)), dma((1,)),
            dma((2, 2)), dma((2, NZ // 2, 4)), dma((2, 2)), dma((2, NZ // 2, 4)),
        ],
        compiler_params=pltpu.CompilerParams(
            collective_id=0, has_side_effects=True, vmem_limit_bytes=55_000_000
        ),
    )(go, si, legendre, quad_weight, mixing_weight)
    return gw, gi.transpose(1, 0, 2)[None]


def solution(mesh):
    in_specs = (
        P("dp", None, "lat", "chan"),
        P("dp", None, "lat", "chan"),
        P("lat", None, None),
        P(),
        P("lat", None, "chan"),
    )
    out_specs = (P("lat", "dp", "chan"), P("dp", None, "lat", "chan"))
    return jax.shard_map(
        on_device, mesh=mesh, in_specs=in_specs, out_specs=out_specs, check_vma=False
    )
```

time: 152 us -> 143 us (0.941)
  the two profiles are of different devices: /device:TPU:8 before, /device:TPU:32 now
where the time goes in v4:
time: 143 us
  Pallas kernels  140 us (98%)
  local copies, waits for them, and re-layouts  2.29 us (2%)
    pallas_call x1, Pallas kernels, on_device(): pl.pallas_call(kernel, out_shape=(jax.ShapeDtypeStruct((LB, Q, Q), BF), j...  140 us

profile of v4, /device:TPU:32, one launch (start us, length us, event | category | flops | bytes accessed | tf_op | source)
XLA Modules:
  0.0 142.7 jit_solution(7485092699830429109)
XLA Ops:
  0.6 0.0 copy-start
  0.6 0.7 copy-done
  1.3 139.7 %shard_map.68 = (bf16[12,128,128]{2,1,0:T(8,128)(2,1)S(1)}, bf16[45,64,128]{2,1,0:T(8,128)(2,1)S(1)}) custom-call(bf16[45,64,128]{2,1,0:T(8,128)(2,1)} %bitcast.10, bf16[45,64,128]{2,1,0:T(8,128)(2,1)} %bitcast.11, bf16[4,192,720]{2,1,0:T(8,128)(2,1)} %leg_in.1, f32[720]{0:T(1024)S(1)} %copy-done, bf16[12,512,128]{2,1,0:T(8,128)(2,1)} %w_in.1), custom_call_target="tpu_custom_call" | custom-call | tf_op jit(solution)/shard_map/pallas_call | solution.py:545
  141.1 0.7 copy.9
  141.8 0.9 copy.10
Async XLA Ops:
  0.6 0.7 copy-start

commit v5 on v4

--- a/solution.py
+++ b/solution.py
@@ -12,6 +12,7 @@
 M, J, Q, LB, MB, CH, NZ = 64, 45, 128, 12, 4, 192, 16
 ROWS = NZ * LB * MB
 NCHAN, NDP = 8, 4
+GROWS = 184
 SHARES = 24
 
 
@@ -54,6 +55,7 @@
     ]
     for load in loads:
         load.start()
+    g1r[:, MB * J - 4 :, :] = jnp.zeros((NZ, CH - MB * J + 4, Q), BF)
 
     def greet_z(s, c):
         to = (z + s + 1) % NZ
@@ -84,6 +86,13 @@
 
         lax.fori_loop(first, last, step, 0)
 
+    def g_copy(to, slot):
+        at = pl.ds(0, GROWS)
+        return pltpu.make_async_remote_copy(
+            src_ref=g1s.at[to, at], dst_ref=g1r.at[slot, at], send_sem=g_ss.at[0],
+            recv_sem=g_rs.at[slot], device_id={"lat": to}, device_id_type=MESH,
+        )
+
     def batch(ref, count, ss, rs):
         at = ref if count is None else ref.at[pl.ds(0, count)]
         return pltpu.make_async_remote_copy(
@@ -94,14 +103,6 @@
     for zz in range(4):
         r, c = iota((CH, 16 * J), 0), iota((CH, 16 * J), 1)
         p_in[pl.ds(zz * CH, CH), :] = one_hot((c == (r // 4) * 16 + zz * 4 + r % 4) & (r < MB * J))
-
-    def order_in(x, out):
-        def step(g, c):
-            rows = x[:, pl.ds(pl.multiple_of(16 * g, 16), 16), :].reshape(16 * J, Q)
-            out[pl.ds(4 * g, 4)] = dot(p_in[...], rows).astype(BF).reshape(4, CH, Q)
-            return c
-
-        lax.fori_loop(0, 4, step, 0)
 
     me = dp * NCHAN + ch
     shares = me < SHARES
@@ -127,16 +128,29 @@
         return c
 
     loads[1].wait()
-    order_in(go, g1s)
     pl.semaphore_wait(barrier, NZ - 1 + NDP * NCHAN - 1)
-    z_send(g1s, g1r, g_ss, g_rs, 0, 1)
+
+    def send_group(i, c):
+        g = (z // 4 + 2 + i) % 4
+        rows = go[:, pl.ds(pl.multiple_of(16 * g, 16), 16), :].reshape(16 * J, Q)
+        g1s[pl.ds(4 * g, 4)] = dot(p_in[...], rows).astype(BF).reshape(4, CH, Q)
+        for u in range(4):
+            to = 4 * g + u
+
+            @pl.when(to != z)
+            def _():
+                g_copy(to, z).start()
+
+        return c
+
+    send_group(0, 0)
     lax.fori_loop(0, NZ // 4, cut, 0)
 
     @pl.when(shares)
     def _():
         z_send(tsend, trecv, t_ss, t_rs, 0, NZ - 1)
 
-    z_send(g1s, g1r, g_ss, g_rs, 1, NZ - 1)
+    lax.fori_loop(1, 4, send_group, 0)
     trecv[z] = tsend[z]
     g1r[z] = g1s[z]
 
@@ -228,11 +242,14 @@
 
     def latitudes(s, c):
         frm = (z + NZ - offset_of(s)) % NZ
-        z_copy(g1s, g1r, g_ss, g_rs, frm, frm).wait_recv()
+        g_copy(frm, frm).wait_recv()
         acc[...] += dot(t_syn[frm], g1r[frm])
         return c
 
-    lax.fori_loop(0, 11, latitudes, 0)
+    lax.fori_loop(0, NZ - 1, latitudes, 0)
+    g2s[...] = acc[...].astype(BF).reshape(NZ, LB * MB, Q)
+    z_send(g2s, g2r, g2_ss, g2_rs, 0, NZ - 1)
+    g2r[z] = g2s[z]
 
     @pl.when(shares)
     def _():
@@ -291,14 +308,6 @@
     for part in range(4):
         p_send(1 - part // 2, 2, part, False)
 
-    lax.fori_loop(11, NZ - 1, latitudes, 0)
-    g2s[...] = acc[...].astype(BF).reshape(NZ, LB * MB, Q)
-    z_send(g2s, g2r, g2_ss, g2_rs, 0, NZ - 1)
-    g2r[z] = g2s[z]
-
-    for part in range(4):
-        p_send(part // 2, 2, part, True)
-    own_terms((z + 6) % NZ, (z + 10) % NZ)
     batch(g2r, NZ - 1, g2_ss.at[0], g2_rs.at[0]).wait_recv()
     grads = dot(p_sort[...], g2r[...].reshape(ROWS, Q)).astype(BF).reshape(LB, M, Q)
     gall[dp] = grads
@@ -325,6 +334,9 @@
     lax.fori_loop(0, NCHAN - 1, k_send, 0)
 
     kr[ch] = ks[ch]
+    for part in range(4):
+        p_send(part // 2, 2, part, True)
+    own_terms((z + 6) % NZ, (z + 10) % NZ)
 
     def ring(hop, c):
         for part in range(4):
@@ -334,7 +346,7 @@
 
         @pl.when(hop == 5)
         def _():
-            batch(g1s, NZ - 1, g_ss.at[0], g_rs.at[0]).wait_send()
+            batch(g1s.at[:, pl.ds(0, GROWS)], NZ - 1, g_ss.at[0], g_rs.at[0]).wait_send()
             batch(g2s, NZ - 1, g2_ss.at[0], g2_rs.at[0]).wait_send()
 
         @pl.when((hop == 6) & shares)

time: 143 us -> 147 us (1.028)
  Pallas kernels: 140 us -> 144 us
    pallas_call x1, Pallas kernels: 140 us -> 144 us  [on_device(): pl.pallas_call(kernel, out_shape=(jax.ShapeDtypeStruct((LB, Q, Q), BF), j...]
where the time goes in v5:
time: 147 us
  Pallas kernels  144 us (98%)
  local copies, waits for them, and re-layouts  2.29 us (2%)
    pallas_call x1, Pallas kernels, on_device(): pl.pallas_call(kernel, out_shape=(jax.ShapeDtypeStruct((LB, Q, Q), BF), j...  144 us

profile of v5, /device:TPU:32, one launch (start us, length us, event | category | flops | bytes accessed | tf_op | source)
XLA Modules:
  0.0 146.8 jit_solution(6864471638872351856)
XLA Ops:
  0.6 0.0 copy-start
  0.6 0.7 copy-done
  1.3 143.9 %shard_map.68 = (bf16[12,128,128]{2,1,0:T(8,128)(2,1)S(1)}, bf16[45,64,128]{2,1,0:T(8,128)(2,1)S(1)}) custom-call(bf16[45,64,128]{2,1,0:T(8,128)(2,1)} %bitcast.10, bf16[45,64,128]{2,1,0:T(8,128)(2,1)} %bitcast.11, bf16[4,192,720]{2,1,0:T(8,128)(2,1)} %leg_in.1, f32[720]{0:T(1024)S(1)} %copy-done, bf16[12,512,128]{2,1,0:T(8,128)(2,1)} %w_in.1), custom_call_target="tpu_custom_call" | custom-call | tf_op jit(solution)/shard_map/pallas_call | solution.py:557
  145.2 0.7 copy.9
  146.0 0.9 copy.10
Async XLA Ops:
  0.6 0.7 copy-start

commit v6 on v5

--- a/solution.py
+++ b/solution.py
@@ -45,7 +45,7 @@
     g1s, g1r, acc, g2s, g2r, gall, sall, ks, kr,
     xa, tsend, trecv, tall, xr, e_col, e_row, keep_f, keep_b, x8, t_f, own, part_r, t_b, ag, oacc, gpart,
     g_ss, g_rs, g2_ss, g2_rs, k_ss, k_rs, d_ss, d_rs, e_ss, e_rs, e1_rs, f_ss,
-    t_ss, t_rs, a_ss, a_rs, p_ss, p_rs, r_ss, r_rs,
+    t_ss, t_rs, a_ss, a_rs, b_ss, b_rs, p_ss, p_rs, r_ss, r_rs,
 ):
     dp, z, ch = lax.axis_index("dp"), lax.axis_index("lat"), lax.axis_index("chan")
     barrier = pltpu.get_barrier_semaphore()
@@ -127,6 +127,7 @@
             tsend[zz] = dot(both, pick).astype(BF)
         return c
 
+    lax.fori_loop(0, NZ // 4, cut, 0)
     loads[1].wait()
     pl.semaphore_wait(barrier, NZ - 1 + NDP * NCHAN - 1)
 
@@ -143,14 +144,11 @@
 
         return c
 
-    send_group(0, 0)
-    lax.fori_loop(0, NZ // 4, cut, 0)
-
     @pl.when(shares)
     def _():
         z_send(tsend, trecv, t_ss, t_rs, 0, NZ - 1)
 
-    lax.fori_loop(1, 4, send_group, 0)
+    lax.fori_loop(0, 4, send_group, 0)
     trecv[z] = tsend[z]
     g1r[z] = g1s[z]
 
@@ -188,23 +186,6 @@
 
     table(r_syn, t_syn)
 
-    def a_copy(to, s):
-        return pltpu.make_async_remote_copy(
-            src_ref=trecv, dst_ref=tall.at[me], send_sem=a_ss.at[s // SHARES], recv_sem=a_rs.at[0],
-            device_id={"dp": to // NCHAN, "chan": to % NCHAN}, device_id_type=MESH,
-        )
-
-    @pl.when(shares)
-    def _():
-        batch(trecv, NZ - 1, t_ss.at[0], t_rs.at[0]).wait_recv()
-
-        def a_send(s, c):
-            a_copy((me + s + 1) % (NDP * NCHAN), s).start()
-            return c
-
-        lax.fori_loop(0, NDP * NCHAN - 1, a_send, 0)
-        tall[me] = trecv[...]
-
     def sort_block(ib, c):
         at = pl.ds(pl.multiple_of(ib * 128, 128), 128)
         r, k = iota((128, ROWS), 0) + ib * 128, iota((128, ROWS), 1)
@@ -236,7 +217,53 @@
         return c
 
     loads[3].wait()
-    lax.fori_loop(0, LB, weave_weight, 0)
+    lax.fori_loop(0, LB // 2, weave_weight, 0)
+
+    core = dp % 2
+    sibling = dp + 1 - 2 * core
+
+    @pl.when(shares)
+    def _():
+        batch(trecv, NZ - 1, t_ss.at[0], t_rs.at[0]).wait_recv()
+
+        def a_send(s, c):
+            to = ((dp // 2) * NCHAN + ch + s + 1) % (2 * NCHAN)
+            pltpu.make_async_remote_copy(
+                src_ref=trecv, dst_ref=tall.at[me], send_sem=a_ss.at[0], recv_sem=a_rs.at[0],
+                device_id={"dp": (to // NCHAN) * 2 + core, "chan": to % NCHAN}, device_id_type=MESH,
+            ).start()
+            return c
+
+        lax.fori_loop(0, 2 * NCHAN - 1, a_send, 0)
+        tall[me] = trecv[...]
+
+    lax.fori_loop(LB // 2, LB, weave_weight, 0)
+
+    def b_copy(first):
+        at = tall.at[pl.ds(first, 8)]
+        return pltpu.make_async_remote_copy(
+            src_ref=at, dst_ref=at, send_sem=b_ss.at[0], recv_sem=b_rs.at[0],
+            device_id={"dp": sibling}, device_id_type=MESH,
+        )
+
+    def to_sibling():
+        @pl.when(core == 0)
+        def _():
+            batch(tall, 15, a_ss.at[0], a_rs.at[0]).wait_recv()
+            b_copy(0).start()
+            b_copy(16).start()
+
+        @pl.when(dp == 1)
+        def _():
+            batch(tall, 7, a_ss.at[0], a_rs.at[0]).wait_recv()
+
+        @pl.when(dp == 3)
+        def _():
+            batch(tall, 8, a_ss.at[0], a_rs.at[0]).wait_recv()
+
+        @pl.when(core == 1)
+        def _():
+            b_copy(8).start()
 
     acc[...] = dot(t_syn[z], g1r[z])
 
@@ -246,18 +273,20 @@
         acc[...] += dot(t_syn[frm], g1r[frm])
         return c
 
-    lax.fori_loop(0, NZ - 1, latitudes, 0)
+    lax.fori_loop(0, 6, latitudes, 0)
+    to_sibling()
+    lax.fori_loop(6, NZ - 1, latitudes, 0)
     g2s[...] = acc[...].astype(BF).reshape(NZ, LB * MB, Q)
     z_send(g2s, g2r, g2_ss, g2_rs, 0, NZ - 1)
     g2r[z] = g2s[z]
 
-    @pl.when(shares)
-    def _():
-        batch(tall, SHARES - 1, a_ss.at[0], a_rs.at[0]).wait_recv()
-
-    @pl.when(jnp.logical_not(shares))
-    def _():
-        batch(tall, None, a_ss.at[0], a_rs.at[0]).wait_recv()
+    @pl.when(core == 0)
+    def _():
+        batch(tall, 8, b_ss.at[0], b_rs.at[0]).wait_recv()
+
+    @pl.when(core == 1)
+    def _():
+        batch(tall, 16, b_ss.at[0], b_rs.at[0]).wait_recv()
 
     rx, cx = iota((128, 64), 0), iota((128, 64), 1)
     spread = one_hot(cx == ((rx % 8) // 2) * 16 + rx // 8)
@@ -327,11 +356,11 @@
             device_id={"chan": to}, device_id_type=MESH,
         )
 
-    def k_send(s, c):
-        k_copy((ch + s + 1) % NCHAN, ch).start()
-        return c
-
-    lax.fori_loop(0, NCHAN - 1, k_send, 0)
+    row, col = ch // 4, ch % 4
+    for u in range(4):
+        k_copy((1 - row) * 4 + (col + u) % 4, ch).start()
+    for u in range(1, 4):
+        k_copy(row * 4 + (col + u) % 4, ch).start()
 
     kr[ch] = ks[ch]
     for part in range(4):
@@ -352,8 +381,15 @@
         @pl.when((hop == 6) & shares)
         def _():
             batch(tsend, NZ - 1, t_ss.at[0], t_rs.at[0]).wait_send()
-            batch(tall, None, a_ss.at[0], a_rs.at[0]).wait_send()
-            batch(tall, NDP * NCHAN - 1 - SHARES, a_ss.at[1], a_rs.at[0]).wait_send()
+            batch(tall, 15, a_ss.at[0], a_rs.at[0]).wait_send()
+
+        @pl.when((hop == 6) & (core == 0))
+        def _():
+            batch(tall, 16, b_ss.at[0], b_rs.at[0]).wait_send()
+
+        @pl.when((hop == 6) & (core == 1))
+        def _():
+            batch(tall, 8, b_ss.at[0], b_rs.at[0]).wait_send()
 
         return c
 
@@ -384,18 +420,7 @@
         for side in range(2):
             r_copy(side, 0, part, z).start()
 
-    def d_copy(to, slot):
-        return pltpu.make_async_remote_copy(
-            src_ref=gall.at[dp], dst_ref=gall.at[slot], send_sem=d_ss.at[0], recv_sem=d_rs.at[0],
-            device_id={"dp": to}, device_id_type=MESH,
-        )
-
-    def d_send(s, c):
-        d_copy((dp + s + 1) % NDP, dp).start()
-        return c
-
-    lax.fori_loop(0, NDP - 1, d_send, 0)
-    home, half, row, col = ch // 2, ch % 2, ch // 4, ch % 4
+    home, half = ch // 2, ch % 2
     relay = (col // 2) == (dp % 2)
     own_relay = home == dp
     mine = sall.at[dp, half]
@@ -424,9 +449,20 @@
         def _():
             e_copy(ks.at[ch], sall.at[dp, half], home, 4 * h + col, e_ss.at[0], e1_rs.at[dp]).start()
 
-    for h in range(2):
-        to = 4 * h + (col + 2) % 4
-        e_copy(ks.at[ch], sall.at[dp, half], home, to, e_ss.at[0], e_rs.at[0]).start()
+    def send_across():
+        for h in range(2):
+            to = 4 * h + (col + 2) % 4
+            e_copy(ks.at[ch], sall.at[dp, half], home, to, e_ss.at[0], e_rs.at[0]).start()
+
+    def d_copy(to, slot):
+        return pltpu.make_async_remote_copy(
+            src_ref=gall.at[dp], dst_ref=gall.at[slot], send_sem=d_ss.at[0], recv_sem=d_rs.at[0],
+            device_id={"dp": to}, device_id_type=MESH,
+        )
+
+    def d_send(s, c):
+        d_copy((dp + s + 1) % NDP, dp).start()
+        return c
 
     @pl.when(own_relay)
     def _():
@@ -481,6 +517,7 @@
 
         @pl.when(k == 2)
         def _():
+            send_across()
             batch(kr, NCHAN - 1, k_ss.at[0], k_rs.at[0]).wait_send()
             for side in range(2):
                 batch(part_r.at[side], 7, p_ss.at[side, 1], p_rs.at[side, 0, 0]).wait_send()
@@ -490,7 +527,11 @@
         def _():
             pass_on()
 
-        @pl.when(k == 5)
+        @pl.when(k == 4)
+        def _():
+            lax.fori_loop(0, NDP - 1, d_send, 0)
+
+        @pl.when(k == 7)
         def _():
             batch(gall, NDP - 1, d_ss.at[0], d_rs.at[0]).wait_recv()
             for b in range(NDP):
@@ -583,7 +624,7 @@
             pltpu.VMEM((NZ, 8, 96, Q), BF), pltpu.VMEM((8, 8 * J, Q), F32),
             pltpu.VMEM((NDP, LB, M, Q), BF),
             dma((1,)), dma((NZ,)), dma((1,)), dma((1,)), dma((1,)), dma((1,)), dma((1,)), dma((1,)),
-            dma((1,)), dma((1,)), dma((NDP,)), dma((1,)), dma((1,)), dma((1,)), dma((2,)), dma((1,)),
+            dma((1,)), dma((1,)), dma((NDP,)), dma((1,)), dma((1,)), dma((1,)), dma((1,)), dma((1,)), dma((1,)), dma((1,)),
             dma((2, 2)), dma((2, NZ // 2, 4)), dma((2, 2)), dma((2, NZ // 2, 4)),
         ],
         compiler_params=pltpu.CompilerParams(

time: 147 us -> 136 us (0.925)
  the two profiles are of different devices: /device:TPU:32 before, /device:TPU:1 now
where the time goes in v6:
time: 136 us; the launch traced here: 134 us
  Pallas kernels  131 us (96%)
  local copies, waits for them, and re-layouts  2.29 us (2%)
    pallas_call x1, Pallas kernels, on_device(): pl.pallas_call(kernel, out_shape=(jax.ShapeDtypeStruct((LB, Q, Q), BF), j...  131 us

profile of v6, /device:TPU:1, one launch (start us, length us, event | category | flops | bytes accessed | tf_op | source)
XLA Modules:
  0.0 133.6 jit_solution(1247621352030659571)
XLA Ops:
  0.6 0.0 copy-start
  0.6 0.7 copy-done
  1.3 130.7 %shard_map.68 = (bf16[12,128,128]{2,1,0:T(8,128)(2,1)S(1)}, bf16[45,64,128]{2,1,0:T(8,128)(2,1)S(1)}) custom-call(bf16[45,64,128]{2,1,0:T(8,128)(2,1)} %bitcast.10, bf16[45,64,128]{2,1,0:T(8,128)(2,1)} %bitcast.11, bf16[4,192,720]{2,1,0:T(8,128)(2,1)} %leg_in.1, f32[720]{0:T(1024)S(1)} %copy-done, bf16[12,512,128]{2,1,0:T(8,128)(2,1)} %w_in.1), custom_call_target="tpu_custom_call" | custom-call | tf_op jit(solution)/shard_map/pallas_call | solution.py:598
  132.0 0.7 copy.9
  132.7 0.9 copy.10
Async XLA Ops:
  0.6 0.7 copy-start

commit v7 on v6

--- a/solution.py
+++ b/solution.py
@@ -12,6 +12,7 @@
 M, J, Q, LB, MB, CH, NZ = 64, 45, 128, 12, 4, 192, 16
 ROWS = NZ * LB * MB
 NCHAN, NDP = 8, 4
+OROWS = 368
 GROWS = 184
 SHARES = 24
 
@@ -198,10 +199,10 @@
 
     r, k = iota((128, 2 * CH), 0), iota((128, 2 * CH), 1)
     e_col[...] = one_hot((r == (k % 2) * 64 + k // 8) & (k < 8 * J))
-    r, k = iota((8 * J, 128), 0), iota((8 * J, 128), 1)
+    r, k = iota((OROWS, 128), 0), iota((OROWS, 128), 1)
     e_row[...] = one_hot(k == (r % 2) * 64 + r // 8)
     keep_f[...] = one_hot(iota((CH, 2 * CH), 0) % 8 == iota((CH, 2 * CH), 1) % 8)
-    keep_b[...] = one_hot(iota((8 * J, CH), 0) % 8 == iota((8 * J, CH), 1) % 8)
+    keep_b[...] = one_hot(iota((OROWS, CH), 0) % 8 == iota((OROWS, CH), 1) % 8)
 
     ra, ca = iota((Q, Q), 0), iota((Q, Q), 1)
     swap = jnp.where(ca == ra + 1, 1.0, 0.0) * jnp.where(ra % 2 == 0, 1.0, 0.0)
@@ -568,7 +569,8 @@
         r_copy(part // 2, NZ // 2 - 1, part, half_way).wait_recv()
         halves = []
         for g in (2 * part, 2 * part + 1):
-            halves.append((oacc[g] + dot(t_b[g, :, :96], ag[half_way, g])).reshape(J, 8, Q))
+            full = oacc[g] + dot(t_b[g, :, :96], ag[half_way, g])
+            halves.append(full[: 8 * J].reshape(J, 8, Q))
         gi[:, pl.ds(16 * part, 16), :] = jnp.concatenate(halves, axis=1).astype(BF)
 
     for side in range(2):
@@ -617,11 +619,11 @@
             pltpu.VMEM((NCHAN, LB, M, Q), BF), pltpu.VMEM((NCHAN, LB, M, Q), BF),
             pltpu.VMEM((2, 16, ROWS), BF), pltpu.VMEM((NZ, 16, 128), BF), pltpu.VMEM((NZ, 16, 128), BF),
             pltpu.VMEM((SHARES, NZ, 16, 128), BF), pltpu.VMEM((8, 8 * CH, 128), BF),
-            pltpu.VMEM((128, 2 * CH), BF), pltpu.VMEM((8 * J, 128), BF),
-            pltpu.VMEM((CH, 2 * CH), BF), pltpu.VMEM((8 * J, CH), BF),
+            pltpu.VMEM((128, 2 * CH), BF), pltpu.VMEM((OROWS, 128), BF),
+            pltpu.VMEM((CH, 2 * CH), BF), pltpu.VMEM((OROWS, CH), BF),
             pltpu.VMEM((8, 2 * CH, Q), BF), pltpu.VMEM((8, CH, 2 * CH), BF), pltpu.VMEM((8, CH, Q), F32),
-            pltpu.VMEM((2, NZ // 2 + 1, 8, 96, Q), BF), pltpu.VMEM((8, 8 * J, CH), BF),
-            pltpu.VMEM((NZ, 8, 96, Q), BF), pltpu.VMEM((8, 8 * J, Q), F32),
+            pltpu.VMEM((2, NZ // 2 + 1, 8, 96, Q), BF), pltpu.VMEM((8, OROWS, CH), BF),
+            pltpu.VMEM((NZ, 8, 96, Q), BF), pltpu.VMEM((8, OROWS, Q), F32),
             pltpu.VMEM((NDP, LB, M, Q), BF),
             dma((1,)), dma((NZ,)), dma((1,)), dma((1,)), dma((1,)), dma((1,)), dma((1,)), dma((1,)),
             dma((1,)), dma((1,)), dma((NDP,)), dma((1,)), dma((1,)), dma((1,)), dma((1,)), dma((1,)), dma((1,)), dma((1,)),

time: 136 us -> 136 us (level)
  no operation moved by 1% of the time
where the time goes in v7:
time: 136 us; the launch traced here: 134 us
  Pallas kernels  131 us (96%)
  local copies, waits for them, and re-layouts  2.29 us (2%)
    pallas_call x1, Pallas kernels, on_device(): pl.pallas_call(kernel, out_shape=(jax.ShapeDtypeStruct((LB, Q, Q), BF), j...  131 us

profile of v7, /device:TPU:1, one launch (start us, length us, event | category | flops | bytes accessed | tf_op | source)
XLA Modules:
  0.0 133.6 jit_solution(11516310079858570988)
XLA Ops:
  0.6 0.0 copy-start
  0.6 0.7 copy-done
  1.3 130.7 %shard_map.68 = (bf16[12,128,128]{2,1,0:T(8,128)(2,1)S(1)}, bf16[45,64,128]{2,1,0:T(8,128)(2,1)S(1)}) custom-call(bf16[45,64,128]{2,1,0:T(8,128)(2,1)} %bitcast.10, bf16[45,64,128]{2,1,0:T(8,128)(2,1)} %bitcast.11, bf16[4,192,720]{2,1,0:T(8,128)(2,1)} %leg_in.1, f32[720]{0:T(1024)S(1)} %copy-done, bf16[12,512,128]{2,1,0:T(8,128)(2,1)} %w_in.1), custom_call_target="tpu_custom_call" | custom-call | tf_op jit(solution)/shard_map/pallas_call | solution.py:600
  132.0 0.7 copy.9
  132.8 0.9 copy.10
Async XLA Ops:
  0.6 0.7 copy-start
